TPU v7x, 256 devices: a whole 4x4x8 slice. The times are simulated.
256 devices in a mesh: seq: 32 (over z, x), tp: 8 (over y, core).
Axes of the slice: x: 4, y: 4, z: 8, core: 2. Of those that a mesh axis runs over, the one named last changes fastest.
Arguments:
- queries: bfloat16 [6144, 6144], P('seq', 'tp'), may hold values from -400 to 400
- key_vectors: bfloat16 [6144, 1024], P('seq', 'tp'), may hold values from -8 to 8
- value_vectors: bfloat16 [6144, 1024], P('seq', 'tp'), may hold values from -6 to 6
- positions: int32 [6144], P('seq'), may hold values from 0 to 6143, as said below
- residual: bfloat16 [6144, 6144], P('seq', 'tp'), may hold values from -200 to 200
- norm_gain: float32 [1, 6144], P(None, 'tp'), may hold values from 0.5 to 1.5
- out_weight: bfloat16 [6144, 6144], P('tp'), may hold values from -0.3125 to 0.3125
Outputs:
- quantized: bfloat16 [6144, 6144], P('seq')
- token_scale: float32 [6144], P('seq')
- new_residual: bfloat16 [6144, 6144], P('seq', 'tp')
Inputs may be any that keep to these rules, and one draw needn't show every extreme that they name: The positions are a permutation of 0 to 6143. Cut into 64 runs of 96 consecutive positions, the rows of one index of seq hold run r in their first 96 rows and run 2 * 32 - 1 - r in their last ones, both in increasing order, with r differing between the indices of seq.
All inputs are finite; a program needn't handle non-finite values. Where the computation divides by a largest or mean magnitude, that divisor is 1e-20 or more.
Results may differ from a plain program's by a relative error of at most 0.012.
Values may be sent and summed in bfloat16 or wider, within the bound.
A program may use at most 64 MiB of HBM per device.

v0:
```python
import math

import jax
import jax.numpy as jnp
from jax import lax
from jax.sharding import Mesh
from jax.sharding import PartitionSpec as P

D = 6144
Q_HEADS = 48
KV_HEADS = 8
HEAD = 128
SEQ = ("seq_0", "seq_1")


NEG_FILL = -1e30


def in_order(tiles, dim):
    dims = list(tiles.shape[1:])
    dims[dim] *= tiles.shape[0]
    return jnp.moveaxis(tiles, 0, dim).reshape(dims)


def sent_to_all(x, axis):
    peers = lax.axis_size(axis)
    return lax.all_to_all(jnp.broadcast_to(x[None], (peers, *x.shape)), axis, 0, 0, tiled=True)


def collect(x, axis, dim):
    return in_order(sent_to_all(x, axis), dim)


def gather_axes(x, axes, dim):
    if not axes:
        return x
    nearer = lax.all_gather(x, axes[-1], axis=dim, tiled=True)
    return gather_axes(nearer, axes[:-1], dim)


def cut_along(x, dim, peers):
    dims = x.shape
    tiles = x.reshape(*dims[:dim], peers, dims[dim] // peers, *dims[dim + 1 :])
    return jnp.moveaxis(tiles, dim, 0)


def summed_on_arrival(x, axis, dim):
    peers = lax.axis_size(axis)
    tiles = lax.all_to_all(cut_along(x, dim, peers), axis, 0, 0, tiled=True)
    return jnp.sum(tiles.astype(jnp.float32), axis=0)


def over_copies(x, axis):
    return sent_to_all(x, axis).sum(axis=0)


def of_everyone(x, axis):
    return sent_to_all(x, axis).max(axis=0)


def fresh_state(kv_count, state_rows):
    return (
        jnp.full((kv_count, state_rows), NEG_FILL, jnp.float32),
        jnp.zeros((kv_count, state_rows), jnp.float32),
        jnp.zeros((kv_count, state_rows, HEAD), jnp.float32),
    )


def attend(state_now, query_part, half_rows_pos, key_block, value_block, key_pos):
    running_max, running_sum, weighted_sum = state_now
    kv_count = query_part.shape[0]
    group_size = Q_HEADS // KV_HEADS
    score_scale = 1.0 / math.sqrt(HEAD)
    query_pos = jnp.tile(half_rows_pos, group_size)
    key_heads = key_block.reshape(key_block.shape[0], kv_count, HEAD)
    value_heads = value_block.reshape(value_block.shape[0], kv_count, HEAD)
    scores = (
        jnp.einsum("kmd,skd->kms", query_part, key_heads, preferred_element_type=jnp.float32)
        * score_scale
    )
    visible = key_pos[None, :] <= query_pos[:, None]
    scores = jnp.where(visible[None], scores, NEG_FILL)
    new_max = jnp.maximum(running_max, jnp.max(scores, axis=2))
    weights = jnp.where(visible[None], jnp.exp(scores - new_max[..., None]), 0.0)
    factor = jnp.exp(running_max - new_max)
    running_sum = running_sum * factor + jnp.sum(weights, axis=2)
    weighted_sum = weighted_sum * factor[..., None] + jnp.einsum(
        "kms,skd->kmd",
        weights.astype(jnp.bfloat16),
        value_heads,
        preferred_element_type=jnp.float32,
    )
    return (new_max, running_sum, weighted_sum)


def fold_block(states, halves, half_pos, key_block, value_block, key_pos):
    result = []
    for half_index in range(2):

        def compute(state_now, half_index=half_index):
            return attend(
                state_now, halves[half_index], half_pos[half_index], key_block, value_block, key_pos
            )

        result.append(compute(states[half_index]))
    return tuple(result)


def fold_piece(states, halves, half_pos, key_piece, value_piece, key_pos):
    row_count = key_piece.shape[0]
    block_rows = math.gcd(row_count, 1024)
    block_count = row_count // block_rows

    def scan_step(loop_carry, block_pair):
        return (
            fold_block(loop_carry, halves, half_pos, block_pair[0], block_pair[1], block_pair[2]),
            None,
        )

    stacked = (
        key_piece.reshape(block_count, block_rows, key_piece.shape[1]),
        value_piece.reshape(block_count, block_rows, value_piece.shape[1]),
        key_pos.reshape(block_count, block_rows),
    )
    states, unused = lax.scan(scan_step, states, stacked)
    return states


def on_device(queries, key_vectors, value_vectors, positions, residual, norm_gain, out_weight):
    token_rows = queries.shape[0]
    run_rows = token_rows // 2
    group_size = Q_HEADS // KV_HEADS
    kv_count = key_vectors.shape[1] // HEAD
    query_split = queries.reshape(2, run_rows, kv_count, group_size, HEAD).transpose(0, 2, 3, 1, 4)
    query_split = query_split.reshape(2, kv_count, group_size * run_rows, HEAD)
    halves = (query_split[0], query_split[1])
    half_pos = (positions[:run_rows], positions[run_rows:])
    initial = (
        fresh_state(kv_count, group_size * run_rows),
        fresh_state(kv_count, group_size * run_rows),
    )
    all_pos = collect(positions, SEQ, 0)
    kv_pair = jnp.stack((key_vectors, value_vectors))
    pieces = gather_axes(kv_pair, SEQ, 1)
    states = fold_piece(initial, halves, half_pos, pieces[0], pieces[1], all_pos)
    outputs = []
    for state_now in states:
        outputs.append((state_now[2] / state_now[1][..., None]).astype(jnp.bfloat16))
    attended = (
        jnp.stack(outputs).reshape(2, kv_count, group_size, run_rows, HEAD).transpose(0, 3, 1, 2, 4)
    )
    attended = attended.reshape(token_rows, kv_count * group_size * HEAD)
    partial_value = jnp.dot(attended, out_weight, preferred_element_type=jnp.float32)
    partial_value = partial_value.astype(jnp.bfloat16).astype(jnp.float32)
    summed = summed_on_arrival(partial_value.astype(jnp.bfloat16), "tp", 1) + residual.astype(
        jnp.float32
    )
    square_sum = over_copies(jnp.sum(summed * summed, axis=1), "tp")
    normed = summed * lax.rsqrt(square_sum / D + 1e-05)[:, None] * norm_gain
    peak_value = of_everyone(jnp.max(jnp.abs(normed), axis=1), "tp") + 1e-06
    local_scaled = (normed / peak_value[:, None]).astype(jnp.bfloat16)
    quantized = collect(local_scaled, "tp", 1)
    new_residual = summed.astype(jnp.bfloat16)
    return (quantized, peak_value, new_residual)


def solution(mesh):
    finer = Mesh(mesh.devices.reshape(8, 4, mesh.shape["tp"]), ("seq_0", "seq_1", "tp"))
    in_specs = (
        P(SEQ, "tp"),
        P(SEQ, "tp"),
        P(SEQ, "tp"),
        P(SEQ),
        P(SEQ, "tp"),
        P(None, "tp"),
        P("tp", None),
    )
    out_specs = (P(SEQ, None), P(SEQ), P(SEQ, "tp"))
    return jax.shard_map(
        on_device, mesh=finer, in_specs=in_specs, out_specs=out_specs, check_vma=False
    )
```

profile of v0, /device:TPU:1, one launch (start us, length us, event | category | flops | bytes accessed | tf_op | source)
XLA Modules:
  0.0 225.7 jit_solution(2265433170640939588)
XLA Ops:
  7.2 0.8 pad_maximum_fusion.1
  8.1 12.3 %all_gather.6 = bf16[2,768,128]{2,1,0:T(8,128)(2,1)} all-gather(bf16[2,192,128]{2,1,0:T(8,128)(2,1)S(1)} %pad_maximum_fusion.1), channel_id=1, replica_groups=mesh['seq_0'=8,'seq_1'=4,'tp'=8] {'seq_1'}, dimensions={1}, use_global_device_ids=true | all-gather | bytes 491520 | tf_op jit(solution)/shard_map/all_gather | solution.py:37
  20.4 1.3 broadcast_in_dim.27
  21.7 9.7 %all-to-all-start = ((s32[32,1,192]{2,1,0:T(1,128)}), s32[32,1,192]{2,1,0:T(1,128)S(1)}, u32[]{:S(2)}, u32[]{:S(2)}) async-start(s32[32,1,192]{2,1,0:T(1,128)} %broadcast_in_dim.27), calls=%async_computation | async-start | bytes 65536 | tf_op jit(solution)/shard_map/all_to_all | solution.py:27
  31.4 1.3 reshape.126
  32.7 0.1 fusion.55
  32.9 7.2 %all-to-all-done = s32[32,1,192]{2,1,0:T(1,128)S(1)} async-done(((s32[32,1,192]{2,1,0:T(1,128)}), s32[32,1,192]{2,1,0:T(1,128)S(1)}, u32[]{:S(2)}, u32[]{:S(2)}) %all-to-all-start) | async-done | bytes 24608 | tf_op jit(solution)/shard_map/all_to_all | solution.py:27
  40.1 0.1 reduce.14
  40.1 0.1 reshape_reshape.3
  40.2 30.0 %all-gather.2.cloned.1.call-done = bf16[2,6144,128]{2,1,0:T(8,128)(2,1)} async-done(((bf16[2,768,128]{2,1,0:T(8,128)(2,1)}), bf16[2,6144,128]{2,1,0:T(8,128)(2,1)}) %all-gather.2.cloned.1.call-update) | async-done | bytes 3145744 | tf_op jit(solution)/shard_map/all_gather | solution.py:37
  70.3 3.7 %fusion.53 = (bf16[1,6144,128]{2,1,0:T(8,128)(2,1)}, bf16[1,6144,128]{2,1,0:T(8,128)(2,1)}) fusion(bf16[2,6144,128]{2,1,0:T(8,128)(2,1)} %all-gather.2.cloned.1.call-done), kind=kLoop, calls=%fused_computation.72 | loop fusion | bytes 6291456 | tf_op jit(solution)/shard_map/slice | solution.py:145
  74.0 51.0 %while.21 = (s32[]{:T(128)}, f32[1,576]{1,0:T(1,128)S(1)}, f32[1,576]{1,0:T(1,128)S(1)}, f32[1,576,128]{2,1,0:T(8,128)S(1)}, f32[1,576]{1,0:T(1,128)S(1)}, /*ind...) while((s32[]{:T(128)}, f32[1,576]{1,0:T(1,128)S(1)}, ...), condition=%wide.region_5.6_spmd.clone, body=%wide.region_0.5_spmd.clone.sunk | while | flops 623303424 | bytes 19169728 | solution.py:125
  74.0 0.1 le.126
  74.1 1.4 fusion.77
  75.5 0.1 le.127
  75.6 1.9 fusion.78
  77.6 1.4 fusion.81
  79.0 1.7 fusion.83
  80.7 1.7 fusion.84
  82.5 0.1 le.126
  82.6 1.4 fusion.77
  84.0 0.1 le.127
  84.1 1.9 fusion.78
  86.1 1.4 fusion.81
  87.5 1.7 fusion.83
  89.2 1.7 fusion.84
  91.1 1.4 fusion.77
  92.6 1.9 fusion.78
  94.6 1.4 fusion.81
  96.0 1.7 fusion.83
  97.7 1.7 fusion.84
  99.6 1.4 fusion.77
  101.1 1.9 fusion.78
  103.1 1.4 fusion.81
  104.5 1.7 fusion.83
  106.2 1.7 fusion.84
  108.1 1.4 fusion.77
  109.6 1.9 fusion.78
  111.6 1.4 fusion.81
  113.0 1.7 fusion.83
  114.7 1.7 fusion.84
  116.5 0.1 le.126
  116.6 1.4 fusion.77
  118.1 1.9 fusion.78
  120.1 1.4 fusion.81
  121.5 1.7 fusion.83
  123.2 1.7 fusion.84
  125.0 0.2 divide_convert_fusion.1
  125.4 0.1 pad_maximum_fusion
  125.5 5.7 %convolution_convert_fusion = bf16[192,6144]{1,0:T(8,128)(2,1)S(1)} fusion(bf16[768,6144]{1,0:T(8,128)(2,1)} %param.15, bf16[24,8,6,128]{3,2,1,0:T(8,128)(2,1)S(1)} %bitcast.126), kind=kOutput, calls=%fused_computation.55 | convolution fusion | flops 1813118976 | bytes 12091392 | tf_op jit(solution)/shard_map/dot_general | solution.py:153
  131.2 0.2 copy.52
  131.3 34.1 %all_to_all.28 = bf16[8,192,768]{2,1,0:T(8,128)(2,1)S(1)} all-to-all(bf16[8,192,768]{2,1,0:T(8,128)(2,1)S(1)} %bitcast.112), channel_id=1, replica_groups=mesh['seq_0'=8,'seq_1'=4,'tp'=8] {'tp'}, dimensions={0} | all-to-all | bytes 4718592 | tf_op jit(solution)/shard_map/all_to_all | solution.py:49
  165.5 0.3 convert_reduce_fusion
  165.8 0.6 copy-done
  166.4 0.2 multiply_reduce_fusion
  166.6 0.6 broadcast_in_dim.28
  167.2 4.3 %all-to-all-start.2 = ((f32[8,1,192]{2,1,0:T(1,128)}), f32[8,1,192]{2,1,0:T(1,128)S(1)}, u32[]{:S(2)}, u32[]{:S(2)}) async-start(f32[8,1,192]{2,1,0:T(1,128)} %broadcast_in_dim.28), calls=%async_computation.2 | async-start | bytes 16384 | tf_op jit(solution)/shard_map/all_to_all | solution.py:27
  171.5 4.6 %all-to-all-done.2 = f32[8,1,192]{2,1,0:T(1,128)S(1)} async-done(((f32[8,1,192]{2,1,0:T(1,128)}), f32[8,1,192]{2,1,0:T(1,128)S(1)}, u32[]{:S(2)}, u32[]{:S(2)}) %all-to-all-start.2) | async-done | bytes 6176 | tf_op jit(solution)/shard_map/all_to_all | solution.py:27
  176.1 0.9 fusion.52
  177.0 7.7 %all_to_all.29 = f32[8,1,192]{2,1,0:T(1,128)S(1)} all-to-all(f32[8,1,192]{2,1,0:T(1,128)S(1)} %broadcast_in_dim.29), channel_id=1, replica_groups=mesh['seq_0'=8,'seq_1'=4,'tp'=8] {'tp'}, dimensions={0} | all-to-all | bytes 12288 | tf_op jit(solution)/shard_map/all_to_all | solution.py:27
  184.7 0.2 divide_convert_fusion
  184.9 0.2 broadcast_in_dim.30
  185.1 32.1 %all_to_all.30 = bf16[8,192,768]{2,1,0:T(8,128)(2,1)S(1)} all-to-all(bf16[8,192,768]{2,1,0:T(8,128)(2,1)S(1)} %broadcast_in_dim.30), channel_id=1, replica_groups=mesh['seq_0'=8,'seq_1'=4,'tp'=8] {'tp'}, dimensions={0} | all-to-all | bytes 4718592 | tf_op jit(solution)/shard_map/all_to_all | solution.py:27
  217.2 1.7 copy.45
  (83 shorter events, 1.5 us)
Async XLA Ops:
  7.2 25.5 %copy-start.2 = (s32[192]{0:T(256)S(1)}, s32[192]{0:T(256)}, u32[]{:S(2)}) copy-start(s32[192]{0:T(256)} %param.12) | copy-start | bytes 2308
  7.2 63.1 %all-gather.2.cloned.1.call-start = ((), (), s32[]{:S(2)}) async-start(), calls=%async_computation.5 | async-start | bytes 3538944 | tf_op jit(solution)/shard_map/all_gather | solution.py:37
  21.7 18.4 %all-to-all-start = ((s32[32,1,192]{2,1,0:T(1,128)}), s32[32,1,192]{2,1,0:T(1,128)S(1)}, u32[]{:S(2)}, u32[]{:S(2)}) async-start(s32[32,1,192]{2,1,0:T(1,128)} %broadcast_in_dim.27), calls=%async_computation | async-start | bytes 65536 | tf_op jit(solution)/shard_map/all_to_all | solution.py:27
  165.5 1.0 copy-start
  165.5 6.0 %copy-start.3 = (f32[1,768]{1,0:T(1,128)S(1)}, f32[1,768]{1,0:T(1,128)}, u32[]{:S(2)}) copy-start(f32[1,768]{1,0:T(1,128)} %param.14) | copy-start | bytes 9220
  167.2 8.9 %all-to-all-start.2 = ((f32[8,1,192]{2,1,0:T(1,128)}), f32[8,1,192]{2,1,0:T(1,128)S(1)}, u32[]{:S(2)}, u32[]{:S(2)}) async-start(f32[8,1,192]{2,1,0:T(1,128)} %broadcast_in_dim.28), calls=%async_computation.2 | async-start | bytes 16384 | tf_op jit(solution)/shard_map/all_to_all | solution.py:27
  184.7 32.5 %copy-start.1 = (f32[192]{0:T(256)}, f32[192]{0:T(256)S(1)}, u32[]{:S(2)}) copy-start(f32[192]{0:T(256)S(1)} %broadcast_add_fusion) | copy-start | bytes 2308
Sparse Core Ops, SparseCore 0:
  20.5 49.7 all-gather.1
where the time goes:
time: 227 us; the launch traced here: 226 us
  blocking collectives  86.2 us (38%)
  matrix products  46.3 us (20%)
  waiting for transfers between devices  41.9 us (18%)
  between operations  14.2 us (6%)
  starting transfers between devices  14 us (6%)
  other arithmetic  11.7 us (5%)
  local copies, waits for them, and re-layouts  11 us (5%)
    all_to_all x2, blocking collectives, sent_to_all(): lax.all_to_all(jnp.broadcast_to(x[None], (peers, *x.shape)), axis, 0, 0,...  39.8 us
    all_to_all x1, blocking collectives, summed_on_arrival(): tiles = lax.all_to_all(cut_along(x, dim, peers), axis, 0, 0, tiled=True)  34.1 us
    all_gather x1, waiting for transfers between devices, gather_axes(): nearer = lax.all_gather(x, axes[-1], axis=dim, tiled=True)  30 us
    dot_general x12, matrix products, attend(): jnp.einsum('kms,skd->kmd', weights.astype(jnp.bfloat16), value_heads, pre...  20.5 us
    dot_general x12, matrix products, attend(): jnp.einsum('kmd,skd->kms', query_part, key_heads, preferred_element_type=...  20.1 us
    all_to_all x2, starting transfers between devices, sent_to_all(): lax.all_to_all(jnp.broadcast_to(x[None], (peers, *x.shape)), axis, 0, 0,...  13.9 us
    all_gather x1, blocking collectives, gather_axes(): nearer = lax.all_gather(x, axes[-1], axis=dim, tiled=True)  12.3 us
    all_to_all x2, waiting for transfers between devices, sent_to_all(): lax.all_to_all(jnp.broadcast_to(x[None], (peers, *x.shape)), axis, 0, 0,...  11.8 us
  transfers between devices with their start and end apart: 3, of which 3 were waited for; matrix products, arithmetic and copies ran while one was open for 1% of the time, Pallas kernels for 0%

commit v1 on v0

v1 whole, which is shorter than its diff:
```python
import functools
import heapq
import math

import jax
import jax.numpy as jnp
from jax import lax
from jax.experimental import pallas as pl
from jax.experimental.pallas import tpu as pltpu
from jax.sharding import PartitionSpec as P

D = 6144
HEADS = 6
HEAD = 128
TOK = 192
RUN = TOK // 2
NX = 4
NZ = 8
ROWS = HEADS * RUN
GROUP = NX * RUN
NEG = -1e30
EXP_SCALE = math.log2(math.e) / math.sqrt(HEAD)
MESH = pl.DeviceIdType.MESH

K_LO, V_LO, K_HI, V_HI, RUN_ID = range(5)
X_FIRST = {K_LO: True, V_LO: False, K_HI: True, V_HI: False, RUN_ID: True}
REACH = {
    K_LO: (2, 1, 4, 3),
    V_LO: (2, 1, 4, 3),
    K_HI: (1, 2, 3, 4),
    V_HI: (1, 2, 3, 4),
    RUN_ID: (2, 1, 4, 3),
}
GROUP_ORDER = (0, 1, -1, 2, -2, 3, -3, 4)


def children(kind, mx, mz):
    xp, xn, zp, zn = REACH[kind]
    along_x, along_z = [], []
    if 0 <= mx < xp:
        along_x.append((kind, mx + 1, mz, 0))
    if -xn < mx <= 0:
        along_x.append((kind, mx - 1, mz, 1))
    if 0 <= mz < zp:
        along_z.append((kind, mx, mz + 1, 2))
    if -zn < mz <= 0:
        along_z.append((kind, mx, mz - 1, 3))
    if X_FIRST[kind]:
        return along_z + along_x if mz == 0 else along_z
    return along_x + along_z if mx == 0 else along_x


def plan():
    latency, piece, tiny = 2.2, 0.55, 0.05
    free = [0.0] * 4
    arrivals = []
    order = []

    def send_all(now, kind, mx, mz):
        for child in children(kind, mx, mz):
            direction = child[3]
            took = tiny if kind == RUN_ID else piece
            free[direction] = max(free[direction], now) + took
            heapq.heappush(arrivals, (free[direction] + latency, child[:3]))

    for kind in (K_LO, V_LO, RUN_ID, K_HI, V_HI):
        send_all(0.0, kind, 0, 0)
    units = []
    for dz in GROUP_ORDER:
        units.append((dz, (K_LO, V_LO, RUN_ID), 0.6))
        units.append((dz, (K_HI, V_HI), 0.4))
    have = set()
    now = 0.5
    steps = []
    for dz, kinds, cost in units:
        needed = set()
        for kind in kinds:
            xp, xn, zp, zn = REACH[kind]
            for mx in range(-xn, xp + 1):
                for mz in range(-zn, zp + 1):
                    if (mz - dz) % NZ == 0 and (mx, mz) != (0, 0):
                        needed.add((kind, mx, mz))
        waits = []
        while arrivals and (not needed <= have or arrivals[0][0] <= now):
            when, key = heapq.heappop(arrivals)
            now = max(now, when)
            have.add(key)
            waits.append(key)
            send_all(now, *key)
        now += cost
        steps.append(waits)
    assert not arrivals
    return steps, now


STEPS, PLANNED_US = plan()
EVENT_ID = {key: i for i, key in enumerate(key for waits in STEPS for key in waits)}
N_EVENTS = len(EVENT_ID)


def update(rows, queries, m_ref, l_ref, acc_ref, keys, values, bias, chunk):
    for start in range(rows[0], rows[1], chunk):
        at = pl.ds(start, chunk)
        scores = lax.dot_general(
            queries[at, :], keys, (((1,), (1,)), ((), ())), preferred_element_type=jnp.float32
        )
        scores = scores * EXP_SCALE
        if bias is not None:
            scores = scores + bias
        width = scores.shape[1]
        old = m_ref[at, :]
        new = jnp.maximum(old, jnp.max(scores, axis=1, keepdims=True))
        factor = jnp.exp2(old - new)
        weights = [
            jnp.exp2(scores[:, i : i + HEAD] - new) for i in range(0, width, HEAD)
        ]
        m_ref[at, :] = new
        l_ref[at, :] = l_ref[at, :] * factor + functools.reduce(jnp.add, weights)
        probs = jnp.concatenate([w.astype(jnp.bfloat16) for w in weights], axis=1)
        acc_ref[at, :] = acc_ref[at, :] * factor + jnp.dot(
            probs, values, preferred_element_type=jnp.float32
        )


def first_block(first, queries, m_ref, l_ref, acc_ref, keys, values):
    at = pl.ds(first, ROWS)
    scores = lax.dot_general(
        queries[at, :], keys, (((1,), (1,)), ((), ())), preferred_element_type=jnp.float32
    )
    scores = (scores * EXP_SCALE).reshape(HEADS, RUN, RUN)
    row = lax.broadcasted_iota(jnp.int32, (HEADS, RUN, RUN), 1)
    column = lax.broadcasted_iota(jnp.int32, (HEADS, RUN, RUN), 2)
    scores = jnp.where(column <= row, scores, NEG).reshape(ROWS, RUN)
    high = jnp.max(scores, axis=1, keepdims=True)
    weights = jnp.exp2(scores - high)
    m_ref[at, :] = jnp.broadcast_to(high, (ROWS, HEAD))
    total = jnp.sum(weights, axis=1, keepdims=True)
    lane = lax.broadcasted_iota(jnp.int32, (ROWS, HEAD), 1)
    l_ref[at, :] = jnp.where(lane == 0, total, 0.0)
    acc_ref[at, :] = jnp.dot(
        weights.astype(jnp.bfloat16), values, preferred_element_type=jnp.float32
    )


def lane_bias(ids, mine, low):
    one = [
        jnp.where(ids[j] < mine if low else ids[j] > mine, 0.0, NEG) for j in range(NX)
    ]
    lane = lax.broadcasted_iota(jnp.int32, (1, HEAD), 1)
    tiles = [
        jnp.where(lane < 96, one[0], one[1]),
        jnp.where(lane < 64, one[1], one[2]),
        jnp.where(lane < 32, one[2], one[3]),
    ]
    return jnp.concatenate(tiles, axis=1)


def attention_kernel(
    q_ref, own_ref, run_ref, swap_ref, out_ref, kv, ids, queries, m_ref, l_ref, acc_ref, send, recv
):
    seq = lax.axis_index("seq")
    tp = lax.axis_index("tp")
    x = lax.rem(seq, NX)
    z = seq // NX
    neighbours = (
        z * NX + lax.rem(x + 1, NX),
        z * NX + lax.rem(x + NX - 1, NX),
        lax.rem(z + 1, NZ) * NX + x,
        lax.rem(z + NZ - 1, NZ) * NX + x,
    )

    def source_of(mx, mz):
        return lax.rem(z + 2 * NZ - mz, NZ) * NX + lax.rem(x + 2 * NX - mx, NX)

    def place(kind, index):
        if kind == RUN_ID:
            return ids.at[index]
        return kv.at[kind, index]

    def copy_to(kind, mx, mz, child):
        own = (mx, mz) == (0, 0)
        index = source_of(mx, mz)
        target = place(kind, index)
        if own:
            source = run_ref.at[0] if kind == RUN_ID else own_ref.at[kind]
        else:
            source = target
        event = EVENT_ID[child[:3]]
        return pltpu.make_async_remote_copy(
            src_ref=source,
            dst_ref=target,
            send_sem=send.at[event],
            recv_sem=recv.at[event],
            device_id=(neighbours[child[3]], tp),
            device_id_type=MESH,
        )

    def send_all(kind, mx, mz):
        for child in children(kind, mx, mz):
            copy_to(kind, mx, mz, child).start()

    def run_events(waits):
        for kind, mx, mz in waits:
            target = place(kind, source_of(mx, mz))
            pltpu.make_async_remote_copy(
                src_ref=target,
                dst_ref=target,
                send_sem=send.at[EVENT_ID[(kind, mx, mz)]],
                recv_sem=recv.at[EVENT_ID[(kind, mx, mz)]],
                device_id=(neighbours[0], tp),
                device_id_type=MESH,
            ).wait_recv()
            send_all(kind, mx, mz)

    barrier = pltpu.get_barrier_semaphore()
    for peer in neighbours:
        pl.semaphore_signal(barrier, inc=1, device_id=(peer, tp), device_id_type=MESH)
    pl.semaphore_wait(barrier, 4)

    for kind in (K_LO, V_LO, RUN_ID, K_HI, V_HI):
        send_all(kind, 0, 0)

    swapped = jnp.broadcast_to(swap_ref[...], (RUN, HEAD)) > 0.5
    for head in range(HEADS):
        columns = pl.ds(head * HEAD, HEAD)
        first = q_ref[pl.ds(0, RUN), columns].astype(jnp.float32)
        last = q_ref[pl.ds(RUN, RUN), columns].astype(jnp.float32)
        queries[pl.ds(head * RUN, RUN), :] = jnp.where(swapped, last, first).astype(jnp.bfloat16)
        queries[pl.ds(ROWS + head * RUN, RUN), :] = jnp.where(swapped, first, last).astype(
            jnp.bfloat16
        )
    for kind in (K_LO, V_LO, K_HI, V_HI):
        kv[kind, seq] = own_ref[kind]
    ids[seq] = run_ref[0]
    mine = run_ref[0]

    first_block(0, queries, m_ref, l_ref, acc_ref, own_ref[K_LO], own_ref[V_LO])
    first_block(ROWS, queries, m_ref, l_ref, acc_ref, own_ref[K_HI], own_ref[V_HI])

    @pl.loop(0, NZ)
    def _(step):
        half = (step + 1) // 2
        dz = jnp.where(lax.rem(step, 2) == 1, half, -half)
        group = lax.rem(z + 2 * NZ - dz, NZ) * NX
        for j in range(NZ):

            @pl.when(step == j)
            def _(j=j):
                run_events(STEPS[2 * j])

        at = pl.ds(group, NX)
        found = ids[at]
        keys = kv[K_LO, at].reshape(GROUP, HEAD)
        values = kv[V_LO, at].reshape(GROUP, HEAD)
        state = (queries, m_ref, l_ref, acc_ref)
        update((0, ROWS), *state, keys, values, lane_bias(found, mine, True), RUN)
        update((ROWS, 2 * ROWS), *state, keys, values, None, RUN)
        for j in range(NZ):

            @pl.when(step == j)
            def _(j=j):
                run_events(STEPS[2 * j + 1])

        keys = kv[K_HI, at].reshape(GROUP, HEAD)
        values = kv[V_HI, at].reshape(GROUP, HEAD)
        update((ROWS, 2 * ROWS), *state, keys, values, lane_bias(found, mine, False), RUN)

    for head in range(HEADS):
        columns = pl.ds(head * HEAD, HEAD)
        parts = []
        for base in (0, ROWS):
            at = pl.ds(base + head * RUN, RUN)
            total = jnp.sum(l_ref[at, :], axis=1, keepdims=True)
            parts.append(acc_ref[at, :] / total)
        low, high = parts
        out_ref[pl.ds(0, RUN), columns] = jnp.where(swapped, high, low).astype(jnp.bfloat16)
        out_ref[pl.ds(RUN, RUN), columns] = jnp.where(swapped, low, high).astype(jnp.bfloat16)

    for kind in (K_LO, V_LO, RUN_ID, K_HI, V_HI):
        xp, xn, zp, zn = REACH[kind]
        for mx in range(-xn, xp + 1):
            for mz in range(-zn, zp + 1):
                for child in children(kind, mx, mz):
                    copy_to(kind, mx, mz, child).wait_send()


def attend(queries, key_vectors, value_vectors, positions):
    swap = positions[0] > positions[RUN]
    low_run = jnp.minimum(positions[0], positions[RUN]) // RUN
    run_row = jnp.full((1, 1, HEAD), low_run, jnp.int32).astype(jnp.float32)
    swap_row = jnp.full((1, HEAD), swap, jnp.int32).astype(jnp.float32)
    lo_k, hi_k = key_vectors[:RUN], key_vectors[RUN:]
    lo_v, hi_v = value_vectors[:RUN], value_vectors[RUN:]
    own = jnp.stack(
        (
            jnp.where(swap, hi_k, lo_k),
            jnp.where(swap, hi_v, lo_v),
            jnp.where(swap, lo_k, hi_k),
            jnp.where(swap, lo_v, hi_v),
        )
    )
    vmem = pl.BlockSpec(memory_space=pltpu.VMEM)
    return pl.pallas_call(
        attention_kernel,
        out_shape=jax.ShapeDtypeStruct((TOK, HEADS * HEAD), jnp.bfloat16),
        in_specs=[vmem] * 4,
        out_specs=vmem,
        scratch_shapes=[
            pltpu.VMEM((4, NX * NZ, RUN, HEAD), jnp.bfloat16),
            pltpu.VMEM((NX * NZ, 1, HEAD), jnp.float32),
            pltpu.VMEM((2 * ROWS, HEAD), jnp.bfloat16),
            pltpu.VMEM((2 * ROWS, HEAD), jnp.float32),
            pltpu.VMEM((2 * ROWS, HEAD), jnp.float32),
            pltpu.VMEM((2 * ROWS, HEAD), jnp.float32),
            pltpu.SemaphoreType.DMA((N_EVENTS,)),
            pltpu.SemaphoreType.DMA((N_EVENTS,)),
        ],
        compiler_params=pltpu.CompilerParams(collective_id=0, has_side_effects=True),
        name="gather_attend",
    )(queries, own, run_row, swap_row)


def in_order(tiles, dim):
    dims = list(tiles.shape[1:])
    dims[dim] *= tiles.shape[0]
    return jnp.moveaxis(tiles, 0, dim).reshape(dims)


def sent_to_all(x, axis):
    peers = lax.axis_size(axis)
    return lax.all_to_all(jnp.broadcast_to(x[None], (peers, *x.shape)), axis, 0, 0, tiled=True)


def cut_along(x, dim, peers):
    dims = x.shape
    tiles = x.reshape(*dims[:dim], peers, dims[dim] // peers, *dims[dim + 1 :])
    return jnp.moveaxis(tiles, dim, 0)


def on_device(queries, key_vectors, value_vectors, positions, residual, norm_gain, out_weight):
    attended = attend(queries, key_vectors, value_vectors, positions)
    partial_value = jnp.dot(attended, out_weight, preferred_element_type=jnp.float32)
    tiles = lax.all_to_all(
        cut_along(partial_value.astype(jnp.bfloat16), 1, 8), "tp", 0, 0, tiled=True
    )
    summed = jnp.sum(tiles.astype(jnp.float32), axis=0) + residual.astype(jnp.float32)
    square_sum = sent_to_all(jnp.sum(summed * summed, axis=1), "tp").sum(axis=0)
    normed = summed * lax.rsqrt(square_sum / D + 1e-05)[:, None] * norm_gain
    peak_value = sent_to_all(jnp.max(jnp.abs(normed), axis=1), "tp").max(axis=0) + 1e-06
    local_scaled = (normed / peak_value[:, None]).astype(jnp.bfloat16)
    quantized = in_order(sent_to_all(local_scaled, "tp"), 1)
    return (quantized, peak_value, summed.astype(jnp.bfloat16))


def solution(mesh):
    in_specs = (
        P("seq", "tp"),
        P("seq", "tp"),
        P("seq", "tp"),
        P("seq"),
        P("seq", "tp"),
        P(None, "tp"),
        P("tp", None),
    )
    out_specs = (P("seq", None), P("seq"), P("seq", "tp"))
    return jax.shard_map(
        on_device, mesh=mesh, in_specs=in_specs, out_specs=out_specs, check_vma=False
    )
```

time: 227 us -> 170 us (0.75)
  Pallas kernels: 0 us -> 65.6 us
  matrix products: 46.3 us -> 5.8 us
  waiting for transfers between devices: 41.9 us -> 4.62 us
  between operations: 14.2 us -> 3.32 us
  starting transfers between devices: 14 us -> 4.28 us
  other arithmetic: 11.7 us -> 3.05 us
  blocking collectives: 86.2 us -> 77.6 us
  local copies, waits for them, and re-layouts: 11 us -> 5.6 us
    pallas_call x0 -> x1, Pallas kernels: none -> 65.6 us  [attend(): pl.pallas_call(attention_kernel, out_shape=jax.ShapeDtypeStruct((TOK, HEA...]
    dot_general x24 -> x0, matrix products: 40.6 us -> none  [the longest x12 20.5 us: attend(): jnp.einsum('kms,skd->kmd', weights.astype(jnp.bfloat16), value_heads, pre...]
    all_gather x1 -> x0, waiting for transfers between devices: 30 us -> none  [gather_axes(): nearer = lax.all_gather(x, axes[-1], axis=dim, tiled=True)]
    all_gather x1 -> x0, blocking collectives: 12.3 us -> none  [gather_axes(): nearer = lax.all_gather(x, axes[-1], axis=dim, tiled=True)]
    all_to_all x2 -> x1, starting transfers between devices: 13.9 us -> 4.28 us  [sent_to_all(): lax.all_to_all(jnp.broadcast_to(x[None], (peers, *x.shape)), axis, 0, 0,...]
    reduce_sum x9 -> x3, other arithmetic: 8.85 us -> 0.51 us  [the longest x1 0.33 us: on_device(): jnp.sum(tiles.astype(jnp.float32), axis=0) + residual.astype(jnp.float32)]
    all_to_all x2 -> x1, waiting for transfers between devices: 11.8 us -> 4.62 us  [sent_to_all(): lax.all_to_all(jnp.broadcast_to(x[None], (peers, *x.shape)), axis, 0, 0,...]
    all_to_all x1, blocking collectives: 34.1 us -> 37.8 us  [on_device(): lax.all_to_all(cut_along(partial_value.astype(jnp.bfloat16), 1, 8), 'tp',...]
  transfers between devices with their start and end apart: 3 -> 1, of which waited for: 3 -> 1; matrix products, arithmetic and copies ran while one was open for 1% -> 0% of each run, Pallas kernels for 0% -> 0%
where the time goes in v1:
time: 170 us
  blocking collectives  77.6 us (46%)
  Pallas kernels  65.6 us (39%)
  matrix products  5.8 us (3%)
  local copies, waits for them, and re-layouts  5.6 us (3%)
  waiting for transfers between devices  4.62 us (3%)
  starting transfers between devices  4.28 us (3%)
  between operations  3.32 us (2%)
  other arithmetic  3.05 us (2%)
    pallas_call x1, Pallas kernels, attend(): pl.pallas_call(attention_kernel, out_shape=jax.ShapeDtypeStruct((TOK, HEA...  65.6 us
    all_to_all x2, blocking collectives, sent_to_all(): lax.all_to_all(jnp.broadcast_to(x[None], (peers, *x.shape)), axis, 0, 0,...  39.8 us
    all_to_all x1, blocking collectives, on_device(): lax.all_to_all(cut_along(partial_value.astype(jnp.bfloat16), 1, 8), 'tp',...  37.8 us
    dot_general x1, matrix products, on_device(): jnp.dot(attended, out_weight, preferred_element_type=jnp.float32)  5.8 us
    all_to_all x1, waiting for transfers between devices, sent_to_all(): lax.all_to_all(jnp.broadcast_to(x[None], (peers, *x.shape)), axis, 0, 0,...  4.62 us
    all_to_all x1, starting transfers between devices, sent_to_all(): lax.all_to_all(jnp.broadcast_to(x[None], (peers, *x.shape)), axis, 0, 0,...  4.28 us
  transfers between devices with their start and end apart: 1, of which 1 were waited for; matrix products, arithmetic and copies ran while one was open for 0% of the time, Pallas kernels for 0%

profile of v1, /device:TPU:1, one launch (start us, length us, event | category | flops | bytes accessed | tf_op | source)
XLA Modules:
  0.0 169.9 jit_solution(5418712106142478985)
XLA Ops:
  0.6 1.3 fusion.1
  4.6 0.8 select_bitcast_fusion.2
  5.4 0.7 pad_maximum_fusion.own_ref
  6.1 0.5 broadcast_in_dim.11.swap_ref
  6.6 0.5 broadcast_in_dim.10.run_ref
  7.1 65.6 %gather_attend.1 = bf16[192,768]{1,0:T(8,128)(2,1)} custom-call(bf16[192,768]{1,0:T(8,128)(2,1)} %q_ref.1, bf16[4,96,128]{2,1,0:T(8,128)(2,1)} %pad_maximum_fusion.own_ref, f32[1,1,128]{2,1,0:T(1,128)} %broadcast_in_dim.10.run_ref, f32[1,128]{1,0:T(1,128)} %broadcast_in_dim.11.swap_ref), custom_call_target="tpu_custom_call" | custom-call | tf_op jit(solution)/shard_map/gather_attend/pallas_call | solution.py:303
  72.7 5.8 %convolution_convert_fusion = bf16[192,6144]{1,0:T(8,128)(2,1)S(1)} fusion(bf16[192,768]{1,0:T(8,128)(2,1)} %gather_attend.1, bf16[768,6144]{1,0:T(8,128)(2,1)} %param.13), kind=kOutput, calls=%fused_computation | convolution fusion | flops 1813118976 | bytes 12091392 | tf_op jit(solution)/shard_map/dot_general | solution.py:342
  78.5 0.2 copy.24
  78.7 37.8 %all_to_all.22 = bf16[8,192,768]{2,1,0:T(8,128)(2,1)S(1)} all-to-all(bf16[8,192,768]{2,1,0:T(8,128)(2,1)S(1)} %bitcast.23), channel_id=1, replica_groups=mesh['seq'=32,'tp'=8] {'tp'}, dimensions={0} | all-to-all | bytes 4718592 | tf_op jit(solution)/shard_map/all_to_all | solution.py:343
  116.5 0.0 copy-start
  116.5 0.0 copy-start.2
  116.5 0.3 convert_reduce_fusion
  116.9 0.6 copy-done
  117.5 0.2 multiply_reduce_fusion
  117.6 0.6 broadcast_in_dim.12
  118.3 4.3 %all-to-all-start.1 = ((f32[8,1,192]{2,1,0:T(1,128)}), f32[8,1,192]{2,1,0:T(1,128)S(1)}, u32[]{:S(2)}, u32[]{:S(2)}) async-start(f32[8,1,192]{2,1,0:T(1,128)} %broadcast_in_dim.12), calls=%async_computation.1 | async-start | bytes 16384 | tf_op jit(solution)/shard_map/all_to_all | solution.py:331
  122.5 0.0 copy-done.2
  122.5 4.6 %all-to-all-done.1 = f32[8,1,192]{2,1,0:T(1,128)S(1)} async-done(((f32[8,1,192]{2,1,0:T(1,128)}), f32[8,1,192]{2,1,0:T(1,128)S(1)}, u32[]{:S(2)}, u32[]{:S(2)}) %all-to-all-start.1) | async-done | bytes 6176 | tf_op jit(solution)/shard_map/all_to_all | solution.py:331
  127.2 0.9 fusion
  128.1 7.7 %all_to_all.23 = f32[8,1,192]{2,1,0:T(1,128)S(1)} all-to-all(f32[8,1,192]{2,1,0:T(1,128)S(1)} %broadcast_in_dim.13), channel_id=1, replica_groups=mesh['seq'=32,'tp'=8] {'tp'}, dimensions={0} | all-to-all | bytes 12288 | tf_op jit(solution)/shard_map/all_to_all | solution.py:331
  135.8 0.0 copy-start.1
  135.8 0.2 divide_convert_fusion
  136.0 0.2 broadcast_in_dim.14
  136.1 32.1 %all_to_all.24 = bf16[8,192,768]{2,1,0:T(8,128)(2,1)S(1)} all-to-all(bf16[8,192,768]{2,1,0:T(8,128)(2,1)S(1)} %broadcast_in_dim.14), channel_id=1, replica_groups=mesh['seq'=32,'tp'=8] {'tp'}, dimensions={0} | all-to-all | bytes 4718592 | tf_op jit(solution)/shard_map/all_to_all | solution.py:331
  168.2 0.0 copy-done.1
  168.2 1.7 copy.22
  (6 shorter events, 0.1 us)
Async XLA Ops:
  116.5 1.0 copy-start
  116.5 6.0 %copy-start.2 = (f32[1,768]{1,0:T(1,128)S(1)}, f32[1,768]{1,0:T(1,128)}, u32[]{:S(2)}) copy-start(f32[1,768]{1,0:T(1,128)} %param.12) | copy-start | bytes 9220
  118.3 8.9 %all-to-all-start.1 = ((f32[8,1,192]{2,1,0:T(1,128)}), f32[8,1,192]{2,1,0:T(1,128)S(1)}, u32[]{:S(2)}, u32[]{:S(2)}) async-start(f32[8,1,192]{2,1,0:T(1,128)} %broadcast_in_dim.12), calls=%async_computation.1 | async-start | bytes 16384 | tf_op jit(solution)/shard_map/all_to_all | solution.py:331
  135.8 32.5 %copy-start.1 = (f32[192]{0:T(256)}, f32[192]{0:T(256)S(1)}, u32[]{:S(2)}) copy-start(f32[192]{0:T(256)S(1)} %broadcast_add_fusion) | copy-start | bytes 2308

commit v2 on v1

--- a/solution.py
+++ b/solution.py
@@ -18,6 +18,13 @@
 NZ = 8
 ROWS = HEADS * RUN
 GROUP = NX * RUN
+CHUNK = 2 * RUN
+COLS = HEADS * HEAD
+HALF = COLS // 2
+N_TP = 8
+NY = 4
+PARTS = 4
+PART = TOK // PARTS
 NEG = -1e30
 EXP_SCALE = math.log2(math.e) / math.sqrt(HEAD)
 MESH = pl.DeviceIdType.MESH
@@ -99,22 +106,29 @@
 
 
 def update(rows, queries, m_ref, l_ref, acc_ref, keys, values, bias, chunk):
-    for start in range(rows[0], rows[1], chunk):
+    starts = range(rows[0], rows[1], chunk)
+    all_scores, all_new, all_factors = [], [], []
+    for start in starts:
+        scores = lax.dot_general(
+            queries[pl.ds(start, chunk), :],
+            keys,
+            (((1,), (1,)), ((), ())),
+            preferred_element_type=jnp.float32,
+        )
+        scores = scores * EXP_SCALE
+        all_scores.append(scores if bias is None else scores + bias)
+    for start, scores in zip(starts, all_scores):
         at = pl.ds(start, chunk)
-        scores = lax.dot_general(
-            queries[at, :], keys, (((1,), (1,)), ((), ())), preferred_element_type=jnp.float32
-        )
-        scores = scores * EXP_SCALE
-        if bias is not None:
-            scores = scores + bias
-        width = scores.shape[1]
         old = m_ref[at, :]
         new = jnp.maximum(old, jnp.max(scores, axis=1, keepdims=True))
-        factor = jnp.exp2(old - new)
+        m_ref[at, :] = new
+        all_new.append(new)
+        all_factors.append(jnp.exp2(old - new))
+    for start, scores, new, factor in zip(starts, all_scores, all_new, all_factors):
+        at = pl.ds(start, chunk)
         weights = [
-            jnp.exp2(scores[:, i : i + HEAD] - new) for i in range(0, width, HEAD)
+            jnp.exp2(scores[:, i : i + HEAD] - new) for i in range(0, scores.shape[1], HEAD)
         ]
-        m_ref[at, :] = new
         l_ref[at, :] = l_ref[at, :] * factor + functools.reduce(jnp.add, weights)
         probs = jnp.concatenate([w.astype(jnp.bfloat16) for w in weights], axis=1)
         acc_ref[at, :] = acc_ref[at, :] * factor + jnp.dot(
@@ -253,8 +267,8 @@
         keys = kv[K_LO, at].reshape(GROUP, HEAD)
         values = kv[V_LO, at].reshape(GROUP, HEAD)
         state = (queries, m_ref, l_ref, acc_ref)
-        update((0, ROWS), *state, keys, values, lane_bias(found, mine, True), RUN)
-        update((ROWS, 2 * ROWS), *state, keys, values, None, RUN)
+        update((0, ROWS), *state, keys, values, lane_bias(found, mine, True), CHUNK)
+        update((ROWS, 2 * ROWS), *state, keys, values, None, CHUNK)
         for j in range(NZ):
 
             @pl.when(step == j)
@@ -263,7 +277,7 @@
 
         keys = kv[K_HI, at].reshape(GROUP, HEAD)
         values = kv[V_HI, at].reshape(GROUP, HEAD)
-        update((ROWS, 2 * ROWS), *state, keys, values, lane_bias(found, mine, False), RUN)
+        update((ROWS, 2 * ROWS), *state, keys, values, lane_bias(found, mine, False), CHUNK)
 
     for head in range(HEADS):
         columns = pl.ds(head * HEAD, HEAD)
@@ -320,36 +334,290 @@
     )(queries, own, run_row, swap_row)
 
 
-def in_order(tiles, dim):
-    dims = list(tiles.shape[1:])
-    dims[dim] *= tiles.shape[0]
-    return jnp.moveaxis(tiles, 0, dim).reshape(dims)
-
-
-def sent_to_all(x, axis):
-    peers = lax.axis_size(axis)
-    return lax.all_to_all(jnp.broadcast_to(x[None], (peers, *x.shape)), axis, 0, 0, tiled=True)
-
-
-def cut_along(x, dim, peers):
-    dims = x.shape
-    tiles = x.reshape(*dims[:dim], peers, dims[dim] // peers, *dims[dim + 1 :])
-    return jnp.moveaxis(tiles, dim, 0)
+FAR = (2, 1, -1, 0)
+ONTO_PARTNER, STEP_UP, STEP_DOWN = range(3)
+(
+    PAIR_0, PAIR_1, PAIR_2, PAIR_3,
+    UP_RELAY, UP_DIRECT, UP_LAST, DOWN_RELAY, DOWN_DIRECT, DOWN_LAST,
+    X_UP, X_DOWN, X_UP_FAR, X_DOWN_FAR,
+    X_PAIR, X_PAIR_UP, X_PAIR_DOWN, X_PAIR_UP_FAR, X_PAIR_DOWN_FAR,
+) = range(19)
+N_ARRIVALS = 19
+
+
+def tail_kernel(
+    att_ref, w_ref, residual_ref, gain_ref,
+    x_ref, new_ref, factor_ref, scale_ref,
+    weights, to_pair, from_pair, mine, outgoing, relayed, got, stats,
+    w_sem, send, recv, stat_send, stat_recv,
+):
+    seq = lax.axis_index("seq")
+    tp = lax.axis_index("tp")
+    core = lax.rem(tp, 2)
+    y = tp // 2
+    peers = (
+        y * 2 + 1 - core,
+        lax.rem(tp + 2, N_TP),
+        lax.rem(tp + 6, N_TP),
+    )
+
+    def block_of(step, parity):
+        return lax.rem(y + step + NY, NY) * 2 + parity
+
+    def columns(step, parity, first=0, width=COLS):
+        return pl.ds(pl.multiple_of(block_of(step, parity) * COLS + first, HEAD), width)
+
+    loads = []
+    for slot in range(8):
+        parity = 1 - core if slot < 4 else core
+        load = pltpu.make_async_copy(
+            w_ref.at[:, columns(FAR[slot % 4], parity)], weights.at[slot], w_sem.at[slot]
+        )
+        load.start()
+        loads.append(load)
+
+    barrier = pltpu.get_barrier_semaphore()
+    for step in range(1, N_TP):
+        pl.semaphore_signal(
+            barrier, inc=1, device_id=(seq, lax.rem(tp + step, N_TP)), device_id_type=MESH
+        )
+    pl.semaphore_wait(barrier, N_TP - 1)
+
+    sent = []
+
+    def ship(part, event, source, target, peer):
+        copy = pltpu.make_async_remote_copy(
+            src_ref=source,
+            dst_ref=target,
+            send_sem=send.at[part, event],
+            recv_sem=recv.at[part, event],
+            device_id=(seq, peers[peer]),
+            device_id_type=MESH,
+        )
+        copy.start()
+        sent.append(copy)
+
+    def await_arrival(part, event, target):
+        pltpu.make_async_remote_copy(
+            src_ref=target,
+            dst_ref=target,
+            send_sem=send.at[part, event],
+            recv_sem=recv.at[part, event],
+            device_id=(seq, peers[0]),
+            device_id_type=MESH,
+        ).wait_recv()
+
+    def rows(part):
+        return pl.ds(part * PART, PART)
+
+    for slot in range(8):
+        loads[slot].wait()
+        product = jnp.dot(att_ref[...], weights[slot], preferred_element_type=jnp.float32)
+        if slot < 4:
+            to_pair[slot] = product.astype(jnp.bfloat16)
+            for part in range(PARTS):
+                ship(
+                    part,
+                    PAIR_0 + slot,
+                    to_pair.at[slot, rows(part)],
+                    from_pair.at[slot, rows(part)],
+                    ONTO_PARTNER,
+                )
+        else:
+            mine[slot - 4] = product
+
+    left = pl.ds(0, HALF)
+    right = pl.ds(HALF, HALF)
+
+    def slab(event, part):
+        return got.at[event - UP_RELAY, rows(part)]
+
+    def pair_sum(part):
+        at = rows(part)
+        for slot, step in enumerate(FAR):
+            await_arrival(part, PAIR_0 + slot, from_pair.at[slot, at])
+            total = mine[slot, at, :] + from_pair[slot, at, :].astype(jnp.float32)
+            if step == 0:
+                mine[slot, at, :] = total
+                continue
+            outgoing[slot, at, :] = total.astype(jnp.bfloat16)
+            here = outgoing.at[slot, at]
+            if step == 2:
+                ship(part, UP_RELAY, here.at[:, left], slab(UP_RELAY, part), STEP_UP)
+                ship(part, DOWN_RELAY, here.at[:, right], slab(DOWN_RELAY, part), STEP_DOWN)
+            elif step == 1:
+                ship(part, UP_DIRECT, here.at[:, right], slab(UP_DIRECT, part), STEP_UP)
+            else:
+                ship(part, DOWN_DIRECT, here.at[:, left], slab(DOWN_DIRECT, part), STEP_DOWN)
+
+    def relay_sum(part):
+        at = rows(part)
+        for way, (arrival, onward, slot, half, peer) in enumerate(
+            (
+                (UP_RELAY, UP_LAST, 1, left, STEP_UP),
+                (DOWN_RELAY, DOWN_LAST, 2, right, STEP_DOWN),
+            )
+        ):
+            await_arrival(part, arrival, slab(arrival, part))
+            total = outgoing[slot, at, half].astype(jnp.float32) + slab(arrival, part)[
+                ...
+            ].astype(jnp.float32)
+            relayed[way, at, :] = total.astype(jnp.bfloat16)
+            ship(part, onward, relayed.at[way, at], slab(onward, part), peer)
+
+    def finish_sum(part):
+        at = rows(part)
+        squares = jnp.zeros((PART, HEAD), jnp.float32)
+        peak = jnp.zeros((PART, HEAD), jnp.float32)
+        for first, direct, last in ((0, DOWN_DIRECT, UP_LAST), (HALF, UP_DIRECT, DOWN_LAST)):
+            half = pl.ds(first, HALF)
+            await_arrival(part, direct, slab(direct, part))
+            await_arrival(part, last, slab(last, part))
+            summed = (
+                mine[3, at, half]
+                + slab(direct, part)[...].astype(jnp.float32)
+                + slab(last, part)[...].astype(jnp.float32)
+                + residual_ref[at, half].astype(jnp.float32)
+            )
+            new_ref[at, half] = summed.astype(jnp.bfloat16)
+            gained = summed * gain_ref[:, half]
+            x_ref[at, columns(0, core, first, HALF)] = gained.astype(jnp.bfloat16)
+            for lane in range(0, HALF, HEAD):
+                piece = summed[:, lane : lane + HEAD]
+                squares = squares + piece * piece
+                peak = jnp.maximum(peak, jnp.abs(gained[:, lane : lane + HEAD]))
+        block = x_ref.at[at, columns(0, core)]
+        ship(part, X_UP, block, block, STEP_UP)
+        ship(part, X_DOWN, block, block, STEP_DOWN)
+        ship(part, X_PAIR, block, block, ONTO_PARTNER)
+        lane = lax.broadcasted_iota(jnp.int32, (PART, HEAD), 1)
+        both = jnp.where(
+            lane == 0,
+            jnp.sum(squares, axis=1, keepdims=True),
+            jnp.max(peak, axis=1, keepdims=True),
+        )
+        both = jnp.concatenate([both, jnp.zeros((HEAD - PART, HEAD), jnp.float32)], axis=0)
+        stats[part, tp] = jnp.transpose(both)[0:8, :]
+        for step in range(1, N_TP):
+            copy = pltpu.make_async_remote_copy(
+                src_ref=stats.at[part, tp],
+                dst_ref=stats.at[part, tp],
+                send_sem=stat_send.at[part, step],
+                recv_sem=stat_recv.at[part, step],
+                device_id=(seq, lax.rem(tp + step, N_TP)),
+                device_id_type=MESH,
+            )
+            copy.start()
+            sent.append(copy)
+
+    def share(part):
+        at = rows(part)
+        for arrival, far, pair, step, first, peer in (
+            (X_UP, X_UP_FAR, X_PAIR_UP, -1, 0, STEP_UP),
+            (X_DOWN, X_DOWN_FAR, X_PAIR_DOWN, 1, HALF, STEP_DOWN),
+        ):
+            block = x_ref.at[at, columns(step, core)]
+            await_arrival(part, arrival, block)
+            half = x_ref.at[at, columns(step, core, first, HALF)]
+            ship(part, far, half, half, peer)
+            ship(part, pair, block, block, ONTO_PARTNER)
+
+    def share_far(part):
+        at = rows(part)
+        for arrival, pair, first in (
+            (X_UP_FAR, X_PAIR_UP_FAR, 0),
+            (X_DOWN_FAR, X_PAIR_DOWN_FAR, HALF),
+        ):
+            half = x_ref.at[at, columns(2, core, first, HALF)]
+            await_arrival(part, arrival, half)
+            ship(part, pair, half, half, ONTO_PARTNER)
+
+    def scales(part):
+        at = rows(part)
+        for step in range(1, N_TP):
+            source = lax.rem(tp + N_TP - step, N_TP)
+            pltpu.make_async_remote_copy(
+                src_ref=stats.at[part, source],
+                dst_ref=stats.at[part, source],
+                send_sem=stat_send.at[part, step],
+                recv_sem=stat_recv.at[part, step],
+                device_id=(seq, peers[0]),
+                device_id_type=MESH,
+            ).wait_recv()
+        total = stats[part, 0, 0:1, :]
+        high = stats[part, 0, 1:2, :]
+        for source in range(1, N_TP):
+            total = total + stats[part, source, 0:1, :]
+            high = jnp.maximum(high, stats[part, source, 1:2, :])
+        root = lax.rsqrt(total / D + 1e-05)
+        scale = high * root + 1e-06
+        scale_ref[part] = scale
+        factor = jnp.transpose(jnp.broadcast_to(root / scale, (HEAD, HEAD)))
+        factor_ref[at, :] = factor[0:PART, :]
+
+    def from_partner(part):
+        at = rows(part)
+        other = 1 - core
+        for event, step, first, width in (
+            (X_PAIR, 0, 0, COLS),
+            (X_PAIR_UP, -1, 0, COLS),
+            (X_PAIR_DOWN, 1, 0, COLS),
+            (X_PAIR_UP_FAR, 2, 0, HALF),
+            (X_PAIR_DOWN_FAR, 2, HALF, HALF),
+        ):
+            await_arrival(part, event, x_ref.at[at, columns(step, other, first, width)])
+
+    stages = (pair_sum, relay_sum, finish_sum, share, share_far, scales, from_partner)
+    for tick in range(PARTS + len(stages) - 1):
+        for depth, stage in enumerate(stages):
+            if 0 <= tick - depth < PARTS:
+                stage(tick - depth)
+    for copy in sent:
+        copy.wait_send()
+
+
+def project_and_share(attended, out_weight, residual, norm_gain):
+    vmem = pl.BlockSpec(memory_space=pltpu.VMEM)
+    bf16, f32 = jnp.bfloat16, jnp.float32
+    return pl.pallas_call(
+        tail_kernel,
+        out_shape=(
+            jax.ShapeDtypeStruct((TOK, D), bf16),
+            jax.ShapeDtypeStruct((TOK, COLS), bf16),
+            jax.ShapeDtypeStruct((TOK, HEAD), f32),
+            jax.ShapeDtypeStruct((PARTS, 1, HEAD), f32),
+        ),
+        in_specs=[vmem, pl.BlockSpec(memory_space=pl.ANY), vmem, vmem],
+        out_specs=[vmem] * 4,
+        scratch_shapes=[
+            pltpu.VMEM((8, COLS, COLS), bf16),
+            pltpu.VMEM((4, TOK, COLS), bf16),
+            pltpu.VMEM((4, TOK, COLS), bf16),
+            pltpu.VMEM((4, TOK, COLS), f32),
+            pltpu.VMEM((3, TOK, COLS), bf16),
+            pltpu.VMEM((2, TOK, HALF), bf16),
+            pltpu.VMEM((6, TOK, HALF), bf16),
+            pltpu.VMEM((PARTS, N_TP, 8, HEAD), f32),
+            pltpu.SemaphoreType.DMA((8,)),
+            pltpu.SemaphoreType.DMA((PARTS, N_ARRIVALS)),
+            pltpu.SemaphoreType.DMA((PARTS, N_ARRIVALS)),
+            pltpu.SemaphoreType.DMA((PARTS, N_TP)),
+            pltpu.SemaphoreType.DMA((PARTS, N_TP)),
+        ],
+        compiler_params=pltpu.CompilerParams(
+            collective_id=1, has_side_effects=True, vmem_limit_bytes=60 * 2**20
+        ),
+        name="project_share",
+    )(attended, out_weight, residual, norm_gain)
 
 
 def on_device(queries, key_vectors, value_vectors, positions, residual, norm_gain, out_weight):
     attended = attend(queries, key_vectors, value_vectors, positions)
-    partial_value = jnp.dot(attended, out_weight, preferred_element_type=jnp.float32)
-    tiles = lax.all_to_all(
-        cut_along(partial_value.astype(jnp.bfloat16), 1, 8), "tp", 0, 0, tiled=True
-    )
-    summed = jnp.sum(tiles.astype(jnp.float32), axis=0) + residual.astype(jnp.float32)
-    square_sum = sent_to_all(jnp.sum(summed * summed, axis=1), "tp").sum(axis=0)
-    normed = summed * lax.rsqrt(square_sum / D + 1e-05)[:, None] * norm_gain
-    peak_value = sent_to_all(jnp.max(jnp.abs(normed), axis=1), "tp").max(axis=0) + 1e-06
-    local_scaled = (normed / peak_value[:, None]).astype(jnp.bfloat16)
-    quantized = in_order(sent_to_all(local_scaled, "tp"), 1)
-    return (quantized, peak_value, summed.astype(jnp.bfloat16))
+    shared, new_residual, factor, scale = project_and_share(
+        attended, out_weight, residual, norm_gain
+    )
+    quantized = (shared.astype(jnp.float32) * factor[:, :1]).astype(jnp.bfloat16)
+    return (quantized, scale[:, 0, :PART].reshape(TOK), new_residual)
 
 
 def solution(mesh):

time: 170 us -> 96.2 us (0.57)
  blocking collectives: 77.6 us -> 0 us
  Pallas kernels: 65.6 us -> 82.7 us
  matrix products: 5.8 us -> 0 us
  waiting for transfers between devices: 4.62 us -> 0 us
  starting transfers between devices: 4.28 us -> 0 us
  other arithmetic: 3.05 us -> 5.08 us
    all_to_all x3 -> x0, blocking collectives: 77.6 us -> none  [the longest x2 39.8 us: sent_to_all(): lax.all_to_all(jnp.broadcast_to(x[None], (peers, *x.shape)), axis, 0, 0,...]
    pallas_call x0 -> x1, Pallas kernels: none -> 42.7 us  [project_and_share(): pl.pallas_call(tail_kernel, out_shape=(jax.ShapeDtypeStruct((TOK, D), bf1...]
    pallas_call x1, Pallas kernels: 65.6 us -> 40 us  [attend(): pl.pallas_call(attention_kernel, out_shape=jax.ShapeDtypeStruct((TOK, HEA...]
    dot_general x1 -> x0, matrix products: 5.8 us -> none  [on_device(): jnp.dot(attended, out_weight, preferred_element_type=jnp.float32)]
    all_to_all x1 -> x0, waiting for transfers between devices: 4.62 us -> none  [sent_to_all(): lax.all_to_all(jnp.broadcast_to(x[None], (peers, *x.shape)), axis, 0, 0,...]
    all_to_all x1 -> x0, starting transfers between devices: 4.28 us -> none  [sent_to_all(): lax.all_to_all(jnp.broadcast_to(x[None], (peers, *x.shape)), axis, 0, 0,...]
    convert_element_type x2 -> x1, other arithmetic: 1.02 us -> 3.63 us  [on_device(): (shared.astype(jnp.float32) * factor[:, :1]).astype(jnp.bfloat16)]
    reshape x2 -> x0, local copies, waits for them, and re-layouts: 1.84 us -> none  [the longest x1 1.68 us: in_order(): return jnp.moveaxis(tiles, 0, dim).reshape(dims)]
  transfers between devices with their start and end apart: 1 -> 0, of which waited for: 1 -> 0; matrix products, arithmetic and copies ran while one was open for 0% -> 0% of each run, Pallas kernels for 0% -> 0%
where the time goes in v2:
time: 96.2 us; the launch traced here: 95.9 us
  Pallas kernels  82.7 us (86%)
  other arithmetic  5.08 us (5%)
  local copies, waits for them, and re-layouts  4.87 us (5%)
  between operations  3.29 us (3%)
    pallas_call x1, Pallas kernels, project_and_share(): pl.pallas_call(tail_kernel, out_shape=(jax.ShapeDtypeStruct((TOK, D), bf1...  42.7 us
    pallas_call x1, Pallas kernels, attend(): pl.pallas_call(attention_kernel, out_shape=jax.ShapeDtypeStruct((TOK, HEA...  40 us
    convert_element_type x1, other arithmetic, on_device(): (shared.astype(jnp.float32) * factor[:, :1]).astype(jnp.bfloat16)  3.63 us

profile of v2, /device:TPU:1, one launch (start us, length us, event | category | flops | bytes accessed | tf_op | source)
XLA Modules:
  0.0 95.9 jit_solution(17237238649007304660)
XLA Ops:
  0.6 1.3 %fusion = (s32[1]{0:T(128)}, s32[1]{0:T(128)}) fusion(s32[192]{0:T(256)} %param.10), kind=kLoop, calls=%fused_computation.8 | loop fusion | bytes 16 | tf_op jit(solution)/shard_map/slice | solution.py:302
  4.6 0.6 broadcast_in_dim.7.swap_ref
  5.2 0.5 broadcast_in_dim.6.run_ref
  5.7 0.8 select_bitcast_fusion.2
  6.5 0.7 pad_maximum_fusion.own_ref
  7.2 40.0 %gather_attend.1.att_ref = bf16[192,768]{1,0:T(8,128)(2,1)} custom-call(bf16[192,768]{1,0:T(8,128)(2,1)} %q_ref.1, bf16[4,96,128]{2,1,0:T(8,128)(2,1)} %pad_maximum_fusion.own_ref, f32[1,1,128]{2,1,0:T(1,128)} %broadcast_in_dim.6.run_ref, f32[1,128]{1,0:T(1,128)} %broadcast_in_dim.7.swap_ref), custom_call_target="tpu_custom_call" | custom-call | tf_op jit(solution)/shard_map/gather_attend/pallas_call | solution.py:317
  47.2 42.7 %project_share.1 = (bf16[192,6144]{1,0:T(8,128)(2,1)}, bf16[192,768]{1,0:T(8,128)(2,1)}, f32[192,128]{1,0:T(8,128)}, f32[4,1,128]{2,1,0:T(1,128)}) custom-call(bf16[192,768]{1,0:T(8,128)(2,1)} %gather_attend.1.att_ref, bf16[768,6144]{1,0:T(8,128)(2,1)} %w_ref.1, bf16[192,768]{1,0:T(8,128)(2,1)} %residual_ref.1, f32[1,768]{1,0:T(1,128)} %gain_ref.1), custom_call_target="tpu_custom_call" | custom-call | tf_op jit(solution)/shard_map/project_share/pallas_call | solution.py:582
  89.8 0.0 copy-start.1
  89.9 0.0 copy-start
  89.9 1.0 %slice_reduce_fusion = f32[192]{0:T(256)S(1)} fusion(f32[192,128]{1,0:T(8,128)} %get-tuple-element.8), kind=kLoop, calls=%fused_computation.2 | loop fusion | bytes 1536 | tf_op jit(solution)/shard_map/slice | solution.py:619
  90.9 3.6 %multiply_convert_fusion = bf16[192,6144]{1,0:T(8,128)(2,1)} fusion(bf16[192,6144]{1,0:T(8,128)(2,1)} %get-tuple-element.7, f32[192]{0:T(256)S(1)} %slice_reduce_fusion), kind=kLoop, calls=%fused_computation | loop fusion | flops 3538944 | bytes 4719360 | tf_op jit(solution)/shard_map/convert_element_type | solution.py:619
  94.5 0.0 copy-done.1
  94.6 0.6 reshape_squeeze.3
  95.2 0.0 copy-done
  95.2 0.7 copy.11
  (1 shorter events, 0.0 us)
Async XLA Ops:
  89.8 4.7 %copy-start.1 = (f32[4,1,128]{2,1,0:T(1,128)S(1)}, f32[4,1,128]{2,1,0:T(1,128)}, u32[]{:S(2)}) copy-start(f32[4,1,128]{2,1,0:T(1,128)} %get-tuple-element.9) | copy-start | bytes 6148
  89.9 5.4 %copy-start = (bf16[192,768]{1,0:T(8,128)(2,1)S(1)}, bf16[192,768]{1,0:T(8,128)(2,1)}, u32[]{:S(2)}) copy-start(bf16[192,768]{1,0:T(8,128)(2,1)} %get-tuple-element.24) | copy-start | bytes 884740

commit v3 on v1

v3 whole, which is shorter than its diff:
```python
import functools
import heapq
import math

import jax
import jax.numpy as jnp
from jax import lax
from jax.experimental import pallas as pl
from jax.experimental.pallas import tpu as pltpu
from jax.sharding import PartitionSpec as P

D = 6144
HEADS = 6
HEAD = 128
TOK = 192
RUN = TOK // 2
NX = 4
NY = 4
NZ = 8
N_TP = 8
ROWS = HEADS * RUN
GROUP = NX * RUN
CHUNK = 2 * RUN
COLS = HEADS * HEAD
HALF = COLS // 2
PER_HALF = 2
PARTS = 2 * PER_HALF
PART = TOK // PARTS
NEG = -1e30
EXP_SCALE = math.log2(math.e) / math.sqrt(HEAD)
MESH = pl.DeviceIdType.MESH

K_LO, V_LO, K_HI, V_HI, RUN_ID = range(5)
KINDS = (K_LO, V_LO, RUN_ID, K_HI, V_HI)
X_FIRST = {K_LO: True, V_LO: False, K_HI: True, V_HI: False, RUN_ID: True}
REACH = {
    K_LO: (2, 1, 4, 3),
    V_LO: (2, 1, 4, 3),
    K_HI: (1, 2, 3, 4),
    V_HI: (1, 2, 3, 4),
    RUN_ID: (2, 1, 4, 3),
}
LO, HI = 0, 1
FAR = (2, 1, -1, 0)
X_PLUS, X_MINUS, Z_PLUS, Z_MINUS, Y_PLUS, Y_MINUS, PAIR = range(7)
(
    UP_RELAY, UP_DIRECT, UP_LAST, DOWN_RELAY, DOWN_DIRECT, DOWN_LAST,
    X_UP, X_DOWN, X_UP_FAR, X_DOWN_FAR,
    X_PAIR, X_PAIR_UP, X_PAIR_DOWN, X_PAIR_UP_FAR, X_PAIR_DOWN_FAR,
) = range(15)
N_ARRIVALS = 15


def children(kind, mx, mz):
    xp, xn, zp, zn = REACH[kind]
    along_x, along_z = [], []
    if 0 <= mx < xp:
        along_x.append((kind, mx + 1, mz, X_PLUS))
    if -xn < mx <= 0:
        along_x.append((kind, mx - 1, mz, X_MINUS))
    if 0 <= mz < zp:
        along_z.append((kind, mx, mz + 1, Z_PLUS))
    if -zn < mz <= 0:
        along_z.append((kind, mx, mz - 1, Z_MINUS))
    if X_FIRST[kind]:
        return along_z + along_x if mz == 0 else along_z
    return along_x + along_z if mx == 0 else along_x


def moves(kind):
    xp, xn, zp, zn = REACH[kind]
    return [
        (kind, mx, mz)
        for mx in range(-xn, xp + 1)
        for mz in range(-zn, zp + 1)
        if (mx, mz) != (0, 0)
    ]


EVENT_ID = {key: i for i, key in enumerate(key for kind in KINDS for key in moves(kind))}
N_EVENTS = len(EVENT_ID)
UNIT_US = 0.6
PROJECT_US = 0.5
HOP_US = 2.3
PAIR_US = 1.1
PIECE_US = 0.55
PART_US = 1.6 * PART / RUN


def plan():
    tasks = {}
    for kind in KINDS:
        took = 0.04 if kind == RUN_ID else PIECE_US
        for key in [(kind, 0, 0)] + moves(kind):
            sends = [(child[:3], child[3], took) for child in children(*key)]
            own = key[1:] == (0, 0)
            rank = (0 if kind in (K_LO, V_LO, RUN_ID) else 1) + (-2 if own else 0)
            tasks[("relay",) + key] = (rank, [] if own else [key], [], 0.03, sends)
    start = [("relay", kind, 0, 0) for kind in KINDS]
    tasks[("diagonal",)] = (2, [], start, 0.8, [])

    def group_keys(kinds, dz):
        return [k for kind in kinds for k in moves(kind) if (k[2] - dz) % NZ == 0]

    lo_kinds, hi_kinds = (K_LO, V_LO, RUN_ID), (K_HI, V_HI)
    fins = {LO: [("diagonal",)], HI: [("diagonal",)]}
    for i, dz in enumerate((0, 1, -1, 2, -2, 3, -3, 4)):
        for name, kinds, half, base in (
            ("lo_lo", lo_kinds, LO, 20),
            ("hi_lo", lo_kinds, HI, 40),
            ("hi_hi", hi_kinds, HI, 41),
        ):
            keys = group_keys(kinds, dz) + (group_keys((RUN_ID,), dz) if name == "hi_hi" else [])
            task = (name, dz)
            relays = [("relay",) + k for k in keys]
            tasks[task] = (base + 0.1 * i, [], relays + [("diagonal",)], UNIT_US, [])
            fins[half].append(task)
    for half in (LO, HI):
        late = 0.5 * half
        parts = range(half * PER_HALF, (half + 1) * PER_HALF)
        tasks[("attended", half)] = (10, [], fins[half], 0.4, [(("att", half), PAIR, 0.3)])
        for slot, step in enumerate(FAR):
            sends = []
            for part in parts:
                if step == 2:
                    sends += [((part, UP_RELAY), Y_PLUS, PART_US), ((part, DOWN_RELAY), Y_MINUS, PART_US)]
                elif step == 1:
                    sends += [((part, UP_DIRECT), Y_PLUS, PART_US)]
                elif step == -1:
                    sends += [((part, DOWN_DIRECT), Y_MINUS, PART_US)]
            needs = [("attended", half)] if slot == 0 else [("project", half, slot - 1)]
            tasks[("project", half, slot)] = (9 + late, [("att", half)], needs, PROJECT_US, sends)
        for part in parts:
            tasks[("pass_up", part)] = (
                4 + late, [(part, UP_RELAY)], [("project", half, 1)], 0.1,
                [((part, UP_LAST), Y_PLUS, PART_US)],
            )
            tasks[("pass_down", part)] = (
                4 + late, [(part, DOWN_RELAY)], [("project", half, 2)], 0.1,
                [((part, DOWN_LAST), Y_MINUS, PART_US)],
            )
            tasks[("finish", part)] = (
                6 + late,
                [(part, e) for e in (UP_DIRECT, DOWN_DIRECT, UP_LAST, DOWN_LAST)],
                [("project", half, 3)],
                0.4,
                [
                    ((part, X_UP), Y_PLUS, 2 * PART_US),
                    ((part, X_DOWN), Y_MINUS, 2 * PART_US),
                    ((part, X_PAIR), PAIR, 0.15),
                    ((part, "stats"), PAIR, 0.1),
                ],
            )
            tasks[("share_up", part)] = (
                5 + late, [(part, X_UP)], [], 0.03,
                [((part, X_UP_FAR), Y_PLUS, PART_US), ((part, X_PAIR_UP), PAIR, 0.15)],
            )
            tasks[("share_down", part)] = (
                5 + late, [(part, X_DOWN)], [], 0.03,
                [((part, X_DOWN_FAR), Y_MINUS, PART_US), ((part, X_PAIR_DOWN), PAIR, 0.15)],
            )
            tasks[("far_up", part)] = (
                5 + late, [(part, X_UP_FAR)], [], 0.03, [((part, X_PAIR_UP_FAR), PAIR, 0.1)]
            )
            tasks[("far_down", part)] = (
                5 + late, [(part, X_DOWN_FAR)], [], 0.03, [((part, X_PAIR_DOWN_FAR), PAIR, 0.1)]
            )
            tasks[("scales", part)] = (50, [(part, "stats")], [("finish", part)], 0.3, [])
            pairs = (X_PAIR, X_PAIR_UP, X_PAIR_DOWN, X_PAIR_UP_FAR, X_PAIR_DOWN_FAR)
            tasks[("collect", part)] = (60, [(part, e) for e in pairs], [], 0.02, [])

    free = [0.0] * 7
    when = {}
    order, done = [], set()
    left = dict(tasks)
    now = 0.0
    while left:
        best = None
        soonest = None
        for task, (rank, arrivals, needs, cost, sends) in left.items():
            if not all(n in done for n in needs) or not all(a in when for a in arrivals):
                continue
            ready = max([when[a] for a in arrivals], default=0.0)
            if ready <= now:
                if best is None or rank < best[0]:
                    best = (rank, task)
            elif soonest is None or ready < soonest:
                soonest = ready
        if best is None:
            now = soonest
            continue
        task = best[1]
        rank, arrivals, needs, cost, sends = left.pop(task)
        now += cost
        done.add(task)
        order.append((task, now))
        for arrival, link, took in sends:
            free[link] = max(free[link], now) + took
            hop = 3.0 if arrival[-1] == "stats" else PAIR_US if link == PAIR else HOP_US
            when[arrival] = free[link] + hop
    return order, now


ORDER, PLANNED_US = plan()


def update(rows, queries, m_ref, l_ref, acc_ref, keys, values, bias, chunk):
    starts = range(rows[0], rows[1], chunk)
    all_scores, all_new, all_factors = [], [], []
    for start in starts:
        scores = lax.dot_general(
            queries[pl.ds(start, chunk), :],
            keys,
            (((1,), (1,)), ((), ())),
            preferred_element_type=jnp.float32,
        )
        scores = scores * EXP_SCALE
        all_scores.append(scores if bias is None else scores + bias)
    for start, scores in zip(starts, all_scores):
        at = pl.ds(start, chunk)
        old = m_ref[at, :]
        new = jnp.maximum(old, jnp.max(scores, axis=1, keepdims=True))
        m_ref[at, :] = new
        all_new.append(new)
        all_factors.append(jnp.exp2(old - new))
    for start, scores, new, factor in zip(starts, all_scores, all_new, all_factors):
        at = pl.ds(start, chunk)
        weights = [
            jnp.exp2(scores[:, i : i + HEAD] - new) for i in range(0, scores.shape[1], HEAD)
        ]
        l_ref[at, :] = l_ref[at, :] * factor + functools.reduce(jnp.add, weights)
        probs = jnp.concatenate([w.astype(jnp.bfloat16) for w in weights], axis=1)
        acc_ref[at, :] = acc_ref[at, :] * factor + jnp.dot(
            probs, values, preferred_element_type=jnp.float32
        )


def first_block(first, queries, m_ref, l_ref, acc_ref, keys, values):
    at = pl.ds(first, ROWS)
    scores = lax.dot_general(
        queries[at, :], keys, (((1,), (1,)), ((), ())), preferred_element_type=jnp.float32
    )
    scores = (scores * EXP_SCALE).reshape(HEADS, RUN, RUN)
    row = lax.broadcasted_iota(jnp.int32, (HEADS, RUN, RUN), 1)
    column = lax.broadcasted_iota(jnp.int32, (HEADS, RUN, RUN), 2)
    scores = jnp.where(column <= row, scores, NEG).reshape(ROWS, RUN)
    high = jnp.max(scores, axis=1, keepdims=True)
    weights = jnp.exp2(scores - high)
    m_ref[at, :] = jnp.broadcast_to(high, (ROWS, HEAD))
    total = jnp.sum(weights, axis=1, keepdims=True)
    lane = lax.broadcasted_iota(jnp.int32, (ROWS, HEAD), 1)
    l_ref[at, :] = jnp.where(lane == 0, total, 0.0)
    acc_ref[at, :] = jnp.dot(
        weights.astype(jnp.bfloat16), values, preferred_element_type=jnp.float32
    )


def lane_bias(ids, mine, low):
    one = [
        jnp.where(ids[j] < mine if low else ids[j] > mine, 0.0, NEG) for j in range(NX)
    ]
    lane = lax.broadcasted_iota(jnp.int32, (1, HEAD), 1)
    tiles = [
        jnp.where(lane < 96, one[0], one[1]),
        jnp.where(lane < 64, one[1], one[2]),
        jnp.where(lane < 32, one[2], one[3]),
    ]
    return jnp.concatenate(tiles, axis=1)


def fused_kernel(
    pos_ref, q_hbm, k_ref, v_ref, w_ref, residual_hbm, gain_ref,
    x_ref, new_ref, factor_ref, scale_ref,
    q_ref, residual_ref, own, own_id, kv, ids, queries, m_ref, l_ref, acc_ref,
    weights, attended, mine, outgoing, relayed, got, stats,
    load_sem, send, recv, w_send, w_recv, att_send, att_recv,
    part_send, part_recv, stat_send, stat_recv,
):
    seq = lax.axis_index("seq")
    tp = lax.axis_index("tp")
    x = lax.rem(seq, NX)
    z = seq // NX
    core = lax.rem(tp, 2)
    y = tp // 2
    peers = (
        (z * NX + lax.rem(x + 1, NX), tp),
        (z * NX + lax.rem(x + NX - 1, NX), tp),
        (lax.rem(z + 1, NZ) * NX + x, tp),
        (lax.rem(z + NZ - 1, NZ) * NX + x, tp),
        (seq, lax.rem(tp + 2, N_TP)),
        (seq, lax.rem(tp + 6, N_TP)),
        (seq, y * 2 + 1 - core),
    )

    def columns(step, parity, first=0, width=COLS):
        block = lax.rem(y + step + NY, NY) * 2 + parity
        return pl.ds(pl.multiple_of(block * COLS + first, HEAD), width)

    sent = []

    def remote(source, target, send_sem, recv_sem, peer):
        return pltpu.make_async_remote_copy(
            src_ref=source,
            dst_ref=target,
            send_sem=send_sem,
            recv_sem=recv_sem,
            device_id=peer,
            device_id_type=MESH,
        )

    def ship(*args):
        copy = remote(*args)
        copy.start()
        sent.append(copy)

    def arrive(target, send_sem, recv_sem):
        remote(target, target, send_sem, recv_sem, peers[PAIR]).wait_recv()

    loads = [
        pltpu.make_async_copy(q_hbm, q_ref, load_sem.at[0]),
        pltpu.make_async_copy(residual_hbm, residual_ref, load_sem.at[1]),
    ]
    for slot, step in enumerate(FAR):
        loads.append(
            pltpu.make_async_copy(
                w_ref.at[:, columns(step, core)],
                weights.at[slot, pl.ds(0, COLS)],
                load_sem.at[2 + slot],
            )
        )
    for load in loads[:2]:
        load.start()

    first, last = pos_ref[0], pos_ref[RUN]
    low_run = jnp.minimum(first, last) // RUN
    mine_id = jnp.full((1, HEAD), low_run, jnp.int32).astype(jnp.float32)
    swapped = jnp.full((RUN, HEAD), jnp.where(first > last, 1, 0), jnp.int32) > 0

    def pick(ref, columns, half):
        one = ref[pl.ds(0, RUN), columns].astype(jnp.float32)
        two = ref[pl.ds(RUN, RUN), columns].astype(jnp.float32)
        return jnp.where(swapped, two, one) if half == LO else jnp.where(swapped, one, two)

    every = pl.ds(0, HEAD)
    for kind, ref, half in ((K_LO, k_ref, LO), (V_LO, v_ref, LO), (K_HI, k_ref, HI), (V_HI, v_ref, HI)):
        piece = pick(ref, every, half).astype(jnp.bfloat16)
        own[kind] = piece
        kv[kind, seq] = piece
    own_id[0] = mine_id
    ids[seq] = mine_id

    barrier = pltpu.get_barrier_semaphore()
    greeted = list(peers[:4]) + [(seq, lax.rem(tp + step, N_TP)) for step in range(1, N_TP)]
    for peer in greeted:
        pl.semaphore_signal(barrier, inc=1, device_id=peer, device_id_type=MESH)
    pl.semaphore_wait(barrier, len(greeted))

    def source_of(mx, mz):
        return lax.rem(z + 2 * NZ - mz, NZ) * NX + lax.rem(x + 2 * NX - mx, NX)

    def place(kind, index):
        return ids.at[index] if kind == RUN_ID else kv.at[kind, index]

    def relay(kind, mx, mz):
        index = source_of(mx, mz)
        here = place(kind, index)
        source = here
        if (mx, mz) == (0, 0):
            source = own_id.at[0] if kind == RUN_ID else own.at[kind]
        else:
            event = EVENT_ID[(kind, mx, mz)]
            arrive(here, send.at[event], recv.at[event])
        for child in children(kind, mx, mz):
            event = EVENT_ID[child[:3]]
            ship(source, here, send.at[event], recv.at[event], peers[child[3]])

    def diagonal():
        for slot in range(4):
            loads[2 + slot].start()
        for slot, step in enumerate(FAR):
            ship(
                w_ref.at[:, columns(step, 1 - core)],
                weights.at[slot, pl.ds(COLS, COLS)],
                w_send.at[slot],
                w_recv.at[slot],
                peers[PAIR],
            )
        loads[0].wait()
        for head in range(HEADS):
            for half in (LO, HI):
                queries[pl.ds(half * ROWS + head * RUN, RUN), :] = pick(
                    q_ref, pl.ds(head * HEAD, HEAD), half
                ).astype(jnp.bfloat16)
        first_block(0, queries, m_ref, l_ref, acc_ref, own[K_LO], own[V_LO])
        first_block(ROWS, queries, m_ref, l_ref, acc_ref, own[K_HI], own[V_HI])

    def unit(dz, half, low_keys):
        at = pl.ds(lax.rem(z + 2 * NZ - dz, NZ) * NX, NX)
        keys = kv[K_LO if low_keys else K_HI, at].reshape(GROUP, HEAD)
        values = kv[V_LO if low_keys else V_HI, at].reshape(GROUP, HEAD)
        bias = None
        if low_keys == (half == LO):
            bias = lane_bias(ids[at], mine_id, low_keys)
        bounds = (half * ROWS, (half + 1) * ROWS)
        update(bounds, queries, m_ref, l_ref, acc_ref, keys, values, bias, CHUNK)

    def attend_half(half):
        for head in range(HEADS):
            at = pl.ds(half * ROWS + head * RUN, RUN)
            total = jnp.sum(l_ref[at, :], axis=1, keepdims=True)
            attended[half, 0, :, pl.ds(head * HEAD, HEAD)] = (acc_ref[at, :] / total).astype(
                jnp.bfloat16
            )
        ship(
            attended.at[half, 0],
            attended.at[half, 1],
            att_send.at[half],
            att_recv.at[half],
            peers[PAIR],
        )

    def rows(part):
        return pl.ds(part * PART, PART)

    left = pl.ds(0, HALF)
    right = pl.ds(HALF, HALF)

    def slab(event, part):
        return got.at[event, rows(part)]

    def send_part(part, event, source, target, peer):
        ship(source, target, part_send.at[part, event], part_recv.at[part, event], peers[peer])

    def await_part(part, event, target):
        arrive(target, part_send.at[part, event], part_recv.at[part, event])

    def project(half, slot):
        if slot == 0:
            arrive(attended.at[half, 1], att_send.at[half], att_recv.at[half])
        if half == LO:
            loads[2 + slot].wait()
            arrive(weights.at[slot, pl.ds(COLS, COLS)], w_send.at[slot], w_recv.at[slot])
        product = jnp.dot(
            attended[half, 0], weights[slot, pl.ds(0, COLS), :], preferred_element_type=jnp.float32
        ) + jnp.dot(
            attended[half, 1],
            weights[slot, pl.ds(COLS, COLS), :],
            preferred_element_type=jnp.float32,
        )
        step = FAR[slot]
        if step == 0:
            mine[pl.ds(half * RUN, RUN), :] = product
            return
        outgoing[slot, pl.ds(half * RUN, RUN), :] = product.astype(jnp.bfloat16)
        for part in range(half * PER_HALF, (half + 1) * PER_HALF):
            here = outgoing.at[slot, rows(part)]
            if step == 2:
                send_part(part, UP_RELAY, here.at[:, left], slab(UP_RELAY, part), Y_PLUS)
                send_part(part, DOWN_RELAY, here.at[:, right], slab(DOWN_RELAY, part), Y_MINUS)
            elif step == 1:
                send_part(part, UP_DIRECT, here.at[:, right], slab(UP_DIRECT, part), Y_PLUS)
            else:
                send_part(part, DOWN_DIRECT, here.at[:, left], slab(DOWN_DIRECT, part), Y_MINUS)

    def pass_on(part, way):
        arrival, onward, slot, half, peer = (
            (UP_RELAY, UP_LAST, 1, left, Y_PLUS),
            (DOWN_RELAY, DOWN_LAST, 2, right, Y_MINUS),
        )[way]
        at = rows(part)
        await_part(part, arrival, slab(arrival, part))
        total = outgoing[slot, at, half].astype(jnp.float32) + slab(arrival, part)[...].astype(
            jnp.float32
        )
        relayed[way, at, :] = total.astype(jnp.bfloat16)
        send_part(part, onward, relayed.at[way, at], slab(onward, part), peer)

    def finish(part):
        at = rows(part)
        half_of = part // PER_HALF
        if part == 0:
            loads[1].wait()
        squares = jnp.zeros((PART, HEAD), jnp.float32)
        peak = jnp.zeros((PART, HEAD), jnp.float32)
        inside = (part % PER_HALF) * PART
        one, two = pl.ds(inside, PART), pl.ds(RUN + inside, PART)
        turned = swapped[0:PART]
        for first, direct, last in ((0, DOWN_DIRECT, UP_LAST), (HALF, UP_DIRECT, DOWN_LAST)):
            await_part(part, direct, slab(direct, part))
            await_part(part, last, slab(last, part))
            for lane in range(0, HALF, HEAD):
                here = pl.ds(first + lane, HEAD)
                there = pl.ds(lane, HEAD)
                low = residual_ref[one, here].astype(jnp.float32)
                high = residual_ref[two, here].astype(jnp.float32)
                old = jnp.where(turned, high, low) if half_of == LO else jnp.where(turned, low, high)
                summed = (
                    mine[at, here]
                    + slab(direct, part)[:, there].astype(jnp.float32)
                    + slab(last, part)[:, there].astype(jnp.float32)
                    + old
                )
                new_ref[at, here] = summed.astype(jnp.bfloat16)
                gained = summed * gain_ref[:, here]
                x_ref[at, columns(0, core, first + lane, HEAD)] = gained.astype(jnp.bfloat16)
                squares = squares + summed * summed
                peak = jnp.maximum(peak, jnp.abs(gained))
        block = x_ref.at[at, columns(0, core)]
        lane = lax.broadcasted_iota(jnp.int32, (PART, HEAD), 1)
        both = jnp.where(
            lane == 0,
            jnp.sum(squares, axis=1, keepdims=True),
            jnp.max(peak, axis=1, keepdims=True),
        )
        if PART < HEAD:
            both = jnp.concatenate([both, jnp.zeros((HEAD - PART, HEAD), jnp.float32)], axis=0)
        stats[part, tp] = jnp.transpose(both)[0:8, :]
        send_part(part, X_UP, block, block, Y_PLUS)
        send_part(part, X_DOWN, block, block, Y_MINUS)
        send_part(part, X_PAIR, block, block, PAIR)
        for step in range(1, N_TP):
            ship(
                stats.at[part, tp],
                stats.at[part, tp],
                stat_send.at[part, step],
                stat_recv.at[part, step],
                (seq, lax.rem(tp + step, N_TP)),
            )

    def share(part, way):
        arrival, far, pair, step, first, peer = (
            (X_UP, X_UP_FAR, X_PAIR_UP, -1, 0, Y_PLUS),
            (X_DOWN, X_DOWN_FAR, X_PAIR_DOWN, 1, HALF, Y_MINUS),
        )[way]
        at = rows(part)
        block = x_ref.at[at, columns(step, core)]
        await_part(part, arrival, block)
        half = x_ref.at[at, columns(step, core, first, HALF)]
        send_part(part, far, half, half, peer)
        send_part(part, pair, block, block, PAIR)

    def share_far(part, way):
        arrival, pair, first = (
            (X_UP_FAR, X_PAIR_UP_FAR, 0),
            (X_DOWN_FAR, X_PAIR_DOWN_FAR, HALF),
        )[way]
        half = x_ref.at[rows(part), columns(2, core, first, HALF)]
        await_part(part, arrival, half)
        send_part(part, pair, half, half, PAIR)

    def scales(part):
        for step in range(1, N_TP):
            source = lax.rem(tp + N_TP - step, N_TP)
            arrive(stats.at[part, source], stat_send.at[part, step], stat_recv.at[part, step])
        total = stats[part, 0, 0:1, :]
        high = stats[part, 0, 1:2, :]
        for source in range(1, N_TP):
            total = total + stats[part, source, 0:1, :]
            high = jnp.maximum(high, stats[part, source, 1:2, :])
        root = lax.rsqrt(total / D + 1e-05)
        scale = high * root + 1e-06
        scale_ref[part] = scale
        factor = jnp.transpose(jnp.broadcast_to(root / scale, (HEAD, HEAD)))
        factor_ref[rows(part), :] = factor[0:PART, :]

    def collect(part):
        at = rows(part)
        other = 1 - core
        for event, step, first, width in (
            (X_PAIR, 0, 0, COLS),
            (X_PAIR_UP, -1, 0, COLS),
            (X_PAIR_DOWN, 1, 0, COLS),
            (X_PAIR_UP_FAR, 2, 0, HALF),
            (X_PAIR_DOWN_FAR, 2, HALF, HALF),
        ):
            await_part(part, event, x_ref.at[at, columns(step, other, first, width)])

    emit = {
        "relay": relay,
        "diagonal": diagonal,
        "lo_lo": lambda dz: unit(dz, LO, True),
        "hi_lo": lambda dz: unit(dz, HI, True),
        "hi_hi": lambda dz: unit(dz, HI, False),
        "attended": attend_half,
        "project": project,
        "pass_up": lambda part: pass_on(part, 0),
        "pass_down": lambda part: pass_on(part, 1),
        "finish": finish,
        "share_up": lambda part: share(part, 0),
        "share_down": lambda part: share(part, 1),
        "far_up": lambda part: share_far(part, 0),
        "far_down": lambda part: share_far(part, 1),
        "scales": scales,
        "collect": collect,
    }
    for task, _ in ORDER:
        emit[task[0]](*task[1:])
    for copy in sent:
        copy.wait_send()


def fused(positions, queries, keys, values, out_weight, residual, gain):
    vmem = pl.BlockSpec(memory_space=pltpu.VMEM)
    hbm = pl.BlockSpec(memory_space=pl.ANY)
    smem = pl.BlockSpec(memory_space=pltpu.SMEM)
    bf16, f32 = jnp.bfloat16, jnp.float32
    dma = pltpu.SemaphoreType.DMA
    return pl.pallas_call(
        fused_kernel,
        out_shape=(
            jax.ShapeDtypeStruct((TOK, D), bf16),
            jax.ShapeDtypeStruct((TOK, COLS), bf16),
            jax.ShapeDtypeStruct((TOK, HEAD), f32),
            jax.ShapeDtypeStruct((PARTS, 1, HEAD), f32),
        ),
        in_specs=[smem, hbm, vmem, vmem, hbm, hbm, vmem],
        out_specs=[vmem] * 4,
        scratch_shapes=[
            pltpu.VMEM((TOK, COLS), bf16),
            pltpu.VMEM((TOK, COLS), bf16),
            pltpu.VMEM((4, RUN, HEAD), bf16),
            pltpu.VMEM((1, 1, HEAD), f32),
            pltpu.VMEM((4, NX * NZ, RUN, HEAD), bf16),
            pltpu.VMEM((NX * NZ, 1, HEAD), f32),
            pltpu.VMEM((2 * ROWS, HEAD), bf16),
            pltpu.VMEM((2 * ROWS, HEAD), f32),
            pltpu.VMEM((2 * ROWS, HEAD), f32),
            pltpu.VMEM((2 * ROWS, HEAD), f32),
            pltpu.VMEM((4, 2 * COLS, COLS), bf16),
            pltpu.VMEM((2, 2, RUN, COLS), bf16),
            pltpu.VMEM((TOK, COLS), f32),
            pltpu.VMEM((3, TOK, COLS), bf16),
            pltpu.VMEM((2, TOK, HALF), bf16),
            pltpu.VMEM((6, TOK, HALF), bf16),
            pltpu.VMEM((PARTS, N_TP, 8, HEAD), f32),
            dma((6,)),
            dma((N_EVENTS,)),
            dma((N_EVENTS,)),
            dma((4,)),
            dma((4,)),
            dma((2,)),
            dma((2,)),
            dma((PARTS, N_ARRIVALS)),
            dma((PARTS, N_ARRIVALS)),
            dma((PARTS, N_TP)),
            dma((PARTS, N_TP)),
        ],
        compiler_params=pltpu.CompilerParams(
            collective_id=0, has_side_effects=True, vmem_limit_bytes=VMEM_LIMIT
        ),
        name="fused",
    )(positions, queries, keys, values, out_weight, residual, gain)


VMEM_LIMIT = 40 * 2**20
WIDTH = 1536


def final_kernel(pos_ref, x_ref, new_ref, factor_ref, scale_ref, out_ref, row_ref, kept_ref):
    first = (pl.program_id(0) == 0) & (pl.program_id(1) == 0)

    @pl.when(first)
    def _():
        swapped = pos_ref[0] > pos_ref[RUN]
        low = jnp.concatenate([scale_ref[i][:, :PART] for i in range(PER_HALF)], axis=1)
        high = jnp.concatenate([scale_ref[i][:, :PART] for i in range(PER_HALF, PARTS)], axis=1)
        turned = jnp.full((1, RUN), jnp.where(swapped, 1, 0), jnp.int32) > 0
        row_ref[...] = jnp.concatenate(
            [jnp.where(turned, high, low), jnp.where(turned, low, high)], axis=1
        )

    kept_ref[...] = new_ref[...]
    factor = factor_ref[...]
    for lane in range(0, WIDTH, HEAD):
        at = pl.ds(lane, HEAD)
        out_ref[:, at] = (x_ref[:, at].astype(jnp.float32) * factor).astype(jnp.bfloat16)


def finalize(positions, x, new, factor, scale):
    def turned(i, pos):
        return jnp.where(pos[0] > pos[RUN], 1 - i, i)

    return pl.pallas_call(
        final_kernel,
        out_shape=(
            jax.ShapeDtypeStruct((TOK, D), jnp.bfloat16),
            jax.ShapeDtypeStruct((1, TOK), jnp.float32),
            jax.ShapeDtypeStruct((TOK, COLS), jnp.bfloat16),
        ),
        grid_spec=pltpu.PrefetchScalarGridSpec(
            num_scalar_prefetch=1,
            grid=(2, D // WIDTH),
            in_specs=[
                pl.BlockSpec((RUN, WIDTH), lambda i, j, pos: (turned(i, pos), j)),
                pl.BlockSpec((RUN, COLS), lambda i, j, pos: (turned(i, pos), 0)),
                pl.BlockSpec((RUN, HEAD), lambda i, j, pos: (turned(i, pos), 0)),
                pl.BlockSpec((PARTS, 1, HEAD), lambda i, j, pos: (0, 0, 0)),
            ],
            out_specs=[
                pl.BlockSpec((RUN, WIDTH), lambda i, j, pos: (i, j)),
                pl.BlockSpec((1, TOK), lambda i, j, pos: (0, 0)),
                pl.BlockSpec((RUN, COLS), lambda i, j, pos: (i, 0)),
            ],
        ),
        compiler_params=pltpu.CompilerParams(vmem_limit_bytes=16 * 2**20),
        name="final",
    )(positions, x, new, factor, scale)


def on_device(queries, key_vectors, value_vectors, positions, residual, norm_gain, out_weight):
    shared, new, factor, scale = fused(
        positions, queries, key_vectors, value_vectors, out_weight, residual, norm_gain
    )
    quantized, row, new_residual = finalize(positions, shared, new, factor, scale)
    return (quantized, row.reshape(TOK), new_residual)


def solution(mesh):
    in_specs = (
        P("seq", "tp"),
        P("seq", "tp"),
        P("seq", "tp"),
        P("seq"),
        P("seq", "tp"),
        P(None, "tp"),
        P("tp", None),
    )
    out_specs = (P("seq", None), P("seq"), P("seq", "tp"))
    return jax.shard_map(
        on_device, mesh=mesh, in_specs=in_specs, out_specs=out_specs, check_vma=False
    )
```

time: 170 us -> 87 us (0.51)
  blocking collectives: 77.6 us -> 0 us
  Pallas kernels: 65.6 us -> 77.4 us
  matrix products: 5.8 us -> 0 us
  waiting for transfers between devices: 4.62 us -> 0 us
  starting transfers between devices: 4.28 us -> 0 us
  other arithmetic: 3.05 us -> 0 us
  local copies, waits for them, and re-layouts: 5.6 us -> 8.55 us
  between operations: 3.32 us -> 0.66 us
    all_to_all x3 -> x0, blocking collectives: 77.6 us -> none  [the longest x2 39.8 us: sent_to_all(): lax.all_to_all(jnp.broadcast_to(x[None], (peers, *x.shape)), axis, 0, 0,...]
    pallas_call x1 -> x2, Pallas kernels: 65.6 us -> 77.4 us  [the longest x1 73.3 us: fused(): pl.pallas_call(fused_kernel, out_shape=(jax.ShapeDtypeStruct((TOK, D), bf...]
    unnamed x6 -> x14, local copies, waits for them, and re-layouts: 0.64 us -> 8.55 us
    dot_general x1 -> x0, matrix products: 5.8 us -> none  [on_device(): jnp.dot(attended, out_weight, preferred_element_type=jnp.float32)]
    all_to_all x1 -> x0, waiting for transfers between devices: 4.62 us -> none  [sent_to_all(): lax.all_to_all(jnp.broadcast_to(x[None], (peers, *x.shape)), axis, 0, 0,...]
    all_to_all x1 -> x0, starting transfers between devices: 4.28 us -> none  [sent_to_all(): lax.all_to_all(jnp.broadcast_to(x[None], (peers, *x.shape)), axis, 0, 0,...]
    reshape x2 -> x0, local copies, waits for them, and re-layouts: 1.84 us -> none  [the longest x1 1.68 us: in_order(): return jnp.moveaxis(tiles, 0, dim).reshape(dims)]
    broadcast_in_dim x5 -> x0, local copies, waits for them, and re-layouts: 1.79 us -> none  [the longest x3 0.77 us: sent_to_all(): jnp.broadcast_to(x[None], (peers, *x.shape))]
  transfers between devices with their start and end apart: 1 -> 0, of which waited for: 1 -> 0; matrix products, arithmetic and copies ran while one was open for 0% -> 0% of each run, Pallas kernels for 0% -> 0%
where the time goes in v3:
time: 87 us; the launch traced here: 86.6 us
  Pallas kernels  77.4 us (89%)
  local copies, waits for them, and re-layouts  8.55 us (10%)
    pallas_call x1, Pallas kernels, fused(): pl.pallas_call(fused_kernel, out_shape=(jax.ShapeDtypeStruct((TOK, D), bf...  73.3 us
    unnamed x14, local copies, waits for them, and re-layouts  8.55 us
    pallas_call x1, Pallas kernels, finalize(): pl.pallas_call(final_kernel, out_shape=(jax.ShapeDtypeStruct((TOK, D), jn...  4.19 us

profile of v3, /device:TPU:1, one launch (start us, length us, event | category | flops | bytes accessed | tf_op | source)
XLA Modules:
  0.0 86.6 jit_solution(15551608238098901580)
XLA Ops:
  0.6 0.0 copy-start
  0.6 3.7 %copy-done = bf16[768,6144]{1,0:T(8,128)(2,1)S(1)} copy-done((bf16[768,6144]{1,0:T(8,128)(2,1)S(1)}, bf16[768,6144]{1,0:T(8,128)(2,1)}, u32[]{:S(2)}) %copy-start) | copy-done | bytes 9437208
  4.3 0.0 copy-start.1
  4.3 1.0 %copy-done.1 = bf16[192,768]{1,0:T(8,128)(2,1)S(1)} copy-done((bf16[192,768]{1,0:T(8,128)(2,1)S(1)}, bf16[192,768]{1,0:T(8,128)(2,1)}, u32[]{:S(2)}) %copy-start.1) | copy-done | bytes 294936
  5.3 0.0 copy-start.2
  5.3 1.0 %copy-done.2 = bf16[192,768]{1,0:T(8,128)(2,1)S(1)} copy-done((bf16[192,768]{1,0:T(8,128)(2,1)S(1)}, bf16[192,768]{1,0:T(8,128)(2,1)}, u32[]{:S(2)}) %copy-start.2) | copy-done | bytes 294936
  6.2 0.0 copy-start.3
  6.2 0.8 copy-done.3
  7.0 0.0 copy-start.4
  7.0 0.8 copy-done.4
  7.8 0.0 copy-start.5
  7.8 0.7 copy-done.5
  8.5 0.0 copy-start.6
  8.5 0.7 copy-done.6
  9.2 73.3 %fused.1 = (bf16[192,6144]{1,0:T(8,128)(2,1)S(1)}, bf16[192,768]{1,0:T(8,128)(2,1)S(1)}, f32[192,128]{1,0:T(8,128)S(1)}, f32[4,1,128]{2,1,0:T(1,128)S(1)}) custom-call(s32[192]{0:T(256)S(1)} %copy-done.5, bf16[192,768]{1,0:T(8,128)(2,1)S(1)} %copy-done.1, bf16[192,128]{1,0:T(8,128)(2,1)S(1)} %copy-done.3, bf16[192,128]{1,0:T(8,128)(2,1)S(1)} %copy-done.4, ...), custom_call_target="tpu_custom_call" | custom-call | tf_op jit(solution)/shard_map/fused/pallas_call | solution.py:608
  82.5 4.2 %final.1 = (bf16[192,6144]{1,0:T(8,128)(2,1)}, f32[1,192]{1,0:T(1,128)}, bf16[192,768]{1,0:T(8,128)(2,1)}) custom-call(s32[192]{0:T(256)S(1)} %copy-done.5, bf16[192,6144]{1,0:T(8,128)(2,1)S(1)} %get-tuple-element.10.x_ref, bf16[192,768]{1,0:T(8,128)(2,1)S(1)} %get-tuple-element.11.new_ref, f32[192,128]{1,0:T(8,128)S(1)} %get-tuple-element.12.factor_ref, ...), custom_call_target="tpu_custom_call" | custom-call | tf_op jit(solution)/shard_map/final/pallas_call | solution.py:683
Async XLA Ops:
  0.6 3.7 %copy-start = (bf16[768,6144]{1,0:T(8,128)(2,1)S(1)}, bf16[768,6144]{1,0:T(8,128)(2,1)}, u32[]{:S(2)}) copy-start(bf16[768,6144]{1,0:T(8,128)(2,1)} %w_ref.1) | copy-start | bytes 28311556
  4.3 1.0 %copy-start.1 = (bf16[192,768]{1,0:T(8,128)(2,1)S(1)}, bf16[192,768]{1,0:T(8,128)(2,1)}, u32[]{:S(2)}) copy-start(bf16[192,768]{1,0:T(8,128)(2,1)} %q_hbm.1) | copy-start | bytes 884740
  5.3 1.0 %copy-start.2 = (bf16[192,768]{1,0:T(8,128)(2,1)S(1)}, bf16[192,768]{1,0:T(8,128)(2,1)}, u32[]{:S(2)}) copy-start(bf16[192,768]{1,0:T(8,128)(2,1)} %residual_hbm.1) | copy-start | bytes 884740
  6.2 0.8 copy-start.3
  7.0 0.8 copy-start.4
  7.8 0.7 copy-start.5
  8.5 0.7 copy-start.6

commit v4 on v3

--- a/solution.py
+++ b/solution.py
@@ -31,7 +31,7 @@
 MESH = pl.DeviceIdType.MESH
 
 K_LO, V_LO, K_HI, V_HI, RUN_ID = range(5)
-KINDS = (K_LO, V_LO, RUN_ID, K_HI, V_HI)
+KINDS = (V_LO, K_LO, RUN_ID, V_HI, K_HI)
 X_FIRST = {K_LO: True, V_LO: False, K_HI: True, V_HI: False, RUN_ID: True}
 REACH = {
     K_LO: (2, 1, 4, 3),
@@ -41,8 +41,11 @@
     RUN_ID: (2, 1, 4, 3),
 }
 LO, HI = 0, 1
+DIRECT = (K_LO, K_HI, RUN_ID, V_LO, V_HI)
+for _k in DIRECT:
+    REACH[_k] = (2, 1) + REACH[_k][2:]
 FAR = (2, 1, -1, 0)
-X_PLUS, X_MINUS, Z_PLUS, Z_MINUS, Y_PLUS, Y_MINUS, PAIR = range(7)
+X_PLUS, X_MINUS, Z_PLUS, Z_MINUS, Y_PLUS, Y_MINUS, PAIR, X_FAR = range(8)
 (
     UP_RELAY, UP_DIRECT, UP_LAST, DOWN_RELAY, DOWN_DIRECT, DOWN_LAST,
     X_UP, X_DOWN, X_UP_FAR, X_DOWN_FAR,
@@ -54,6 +57,10 @@
 def children(kind, mx, mz):
     xp, xn, zp, zn = REACH[kind]
     along_x, along_z = [], []
+    if kind in DIRECT and mx == 0:
+        along_x = [(kind, 1, mz, X_PLUS), (kind, -1, mz, X_MINUS), (kind, 2, mz, X_FAR)]
+    if kind in DIRECT:
+        xp = xn = 0
     if 0 <= mx < xp:
         along_x.append((kind, mx + 1, mz, X_PLUS))
     if -xn < mx <= 0:
@@ -165,11 +172,17 @@
             tasks[("far_down", part)] = (
                 5 + late, [(part, X_DOWN_FAR)], [], 0.03, [((part, X_PAIR_DOWN_FAR), PAIR, 0.1)]
             )
-            tasks[("scales", part)] = (50, [(part, "stats")], [("finish", part)], 0.3, [])
+            tasks[("scales", part)] = (
+                50,
+                [(part, "stats")],
+                [(far, every) for far in ("far_up", "far_down") for every in range(PARTS)],
+                0.3,
+                [],
+            )
             pairs = (X_PAIR, X_PAIR_UP, X_PAIR_DOWN, X_PAIR_UP_FAR, X_PAIR_DOWN_FAR)
             tasks[("collect", part)] = (60, [(part, e) for e in pairs], [], 0.02, [])
 
-    free = [0.0] * 7
+    free = [0.0] * 8
     when = {}
     order, done = [], set()
     left = dict(tasks)
@@ -195,6 +208,11 @@
         done.add(task)
         order.append((task, now))
         for arrival, link, took in sends:
+            if link == X_FAR:
+                free[X_PLUS] = max(free[X_PLUS], now) + took
+                free[X_MINUS] = max(free[X_MINUS], now) + took
+                when[arrival] = max(free[X_PLUS], free[X_MINUS]) + HOP_US + 0.7
+                continue
             free[link] = max(free[link], now) + took
             hop = 3.0 if arrival[-1] == "stats" else PAIR_US if link == PAIR else HOP_US
             when[arrival] = free[link] + hop
@@ -269,11 +287,11 @@
 
 
 def fused_kernel(
-    pos_ref, q_hbm, k_ref, v_ref, w_ref, residual_hbm, gain_ref,
-    x_ref, new_ref, factor_ref, scale_ref,
-    q_ref, residual_ref, own, own_id, kv, ids, queries, m_ref, l_ref, acc_ref,
+    pos_hbm, q_hbm, k_hbm, v_hbm, w_ref, residual_hbm, gain_hbm,
+    x_hbm, new_ref, factor_ref, scale_ref, turn_ref,
+    x_ref, pos_ref, q_ref, k_ref, v_ref, residual_ref, gain_ref, own, own_id, kv, ids, queries, m_ref, l_ref, acc_ref,
     weights, attended, mine, outgoing, relayed, got, stats,
-    load_sem, send, recv, w_send, w_recv, att_send, att_recv,
+    store_sem, early_sem, load_sem, send, recv, w_send, w_recv, att_send, att_recv,
     part_send, part_recv, stat_send, stat_recv,
 ):
     seq = lax.axis_index("seq")
@@ -290,6 +308,7 @@
         (seq, lax.rem(tp + 2, N_TP)),
         (seq, lax.rem(tp + 6, N_TP)),
         (seq, y * 2 + 1 - core),
+        (z * NX + lax.rem(x + 2, NX), tp),
     )
 
     def columns(step, parity, first=0, width=COLS):
@@ -297,6 +316,7 @@
         return pl.ds(pl.multiple_of(block * COLS + first, HEAD), width)
 
     sent = []
+    stores = []
 
     def remote(source, target, send_sem, recv_sem, peer):
         return pltpu.make_async_remote_copy(
@@ -328,8 +348,21 @@
                 load_sem.at[2 + slot],
             )
         )
-    for load in loads[:2]:
+    early = [
+        pltpu.make_async_copy(k_hbm, k_ref, early_sem.at[0]),
+        pltpu.make_async_copy(v_hbm, v_ref, early_sem.at[1]),
+        pltpu.make_async_copy(pos_hbm, pos_ref, early_sem.at[2]),
+        pltpu.make_async_copy(gain_hbm, gain_ref, early_sem.at[3]),
+    ]
+    for load in early + loads[:2]:
         load.start()
+
+    barrier = pltpu.get_barrier_semaphore()
+    greeted = list(peers[:4]) + [peers[X_FAR]] + [(seq, lax.rem(tp + step, N_TP)) for step in range(1, N_TP)]
+    for peer in greeted:
+        pl.semaphore_signal(barrier, inc=1, device_id=peer, device_id_type=MESH)
+    for load in early:
+        load.wait()
 
     first, last = pos_ref[0], pos_ref[RUN]
     low_run = jnp.minimum(first, last) // RUN
@@ -346,13 +379,10 @@
         piece = pick(ref, every, half).astype(jnp.bfloat16)
         own[kind] = piece
         kv[kind, seq] = piece
+    turn_ref[...] = swapped[0:1].astype(jnp.float32)
     own_id[0] = mine_id
     ids[seq] = mine_id
 
-    barrier = pltpu.get_barrier_semaphore()
-    greeted = list(peers[:4]) + [(seq, lax.rem(tp + step, N_TP)) for step in range(1, N_TP)]
-    for peer in greeted:
-        pl.semaphore_signal(barrier, inc=1, device_id=peer, device_id_type=MESH)
     pl.semaphore_wait(barrier, len(greeted))
 
     def source_of(mx, mz):
@@ -574,6 +604,9 @@
             (X_PAIR_DOWN_FAR, 2, HALF, HALF),
         ):
             await_part(part, event, x_ref.at[at, columns(step, other, first, width)])
+        store = pltpu.make_async_copy(x_ref.at[at], x_hbm.at[at], store_sem.at[part])
+        store.start()
+        stores.append(store)
 
     emit = {
         "relay": relay,
@@ -597,12 +630,13 @@
         emit[task[0]](*task[1:])
     for copy in sent:
         copy.wait_send()
+    for store in stores:
+        store.wait()
 
 
 def fused(positions, queries, keys, values, out_weight, residual, gain):
     vmem = pl.BlockSpec(memory_space=pltpu.VMEM)
-    hbm = pl.BlockSpec(memory_space=pl.ANY)
-    smem = pl.BlockSpec(memory_space=pltpu.SMEM)
+    hbm = pl.BlockSpec(memory_space=pltpu.HBM)
     bf16, f32 = jnp.bfloat16, jnp.float32
     dma = pltpu.SemaphoreType.DMA
     return pl.pallas_call(
@@ -612,12 +646,18 @@
             jax.ShapeDtypeStruct((TOK, COLS), bf16),
             jax.ShapeDtypeStruct((TOK, HEAD), f32),
             jax.ShapeDtypeStruct((PARTS, 1, HEAD), f32),
+            jax.ShapeDtypeStruct((1, HEAD), f32),
         ),
-        in_specs=[smem, hbm, vmem, vmem, hbm, hbm, vmem],
-        out_specs=[vmem] * 4,
+        in_specs=[hbm] * 7,
+        out_specs=[hbm] + [vmem] * 4,
         scratch_shapes=[
+            pltpu.VMEM((TOK, D), bf16),
+            pltpu.SMEM((TOK,), jnp.int32),
             pltpu.VMEM((TOK, COLS), bf16),
+            pltpu.VMEM((TOK, HEAD), bf16),
+            pltpu.VMEM((TOK, HEAD), bf16),
             pltpu.VMEM((TOK, COLS), bf16),
+            pltpu.VMEM((1, COLS), f32),
             pltpu.VMEM((4, RUN, HEAD), bf16),
             pltpu.VMEM((1, 1, HEAD), f32),
             pltpu.VMEM((4, NX * NZ, RUN, HEAD), bf16),
@@ -633,6 +673,8 @@
             pltpu.VMEM((2, TOK, HALF), bf16),
             pltpu.VMEM((6, TOK, HALF), bf16),
             pltpu.VMEM((PARTS, N_TP, 8, HEAD), f32),
+            dma((PARTS,)),
+            dma((4,)),
             dma((6,)),
             dma((N_EVENTS,)),
             dma((N_EVENTS,)),
@@ -652,34 +694,74 @@
     )(positions, queries, keys, values, out_weight, residual, gain)
 
 
-VMEM_LIMIT = 40 * 2**20
-WIDTH = 1536
-
-
-def final_kernel(pos_ref, x_ref, new_ref, factor_ref, scale_ref, out_ref, row_ref, kept_ref):
-    first = (pl.program_id(0) == 0) & (pl.program_id(1) == 0)
-
-    @pl.when(first)
-    def _():
-        swapped = pos_ref[0] > pos_ref[RUN]
-        low = jnp.concatenate([scale_ref[i][:, :PART] for i in range(PER_HALF)], axis=1)
-        high = jnp.concatenate([scale_ref[i][:, :PART] for i in range(PER_HALF, PARTS)], axis=1)
-        turned = jnp.full((1, RUN), jnp.where(swapped, 1, 0), jnp.int32) > 0
-        row_ref[...] = jnp.concatenate(
-            [jnp.where(turned, high, low), jnp.where(turned, low, high)], axis=1
+VMEM_LIMIT = 67043328
+STRIP = 32
+
+
+def final_kernel(
+    x_hbm, new_hbm, factor_hbm, scale_hbm, turn_hbm, out_hbm, row_ref, kept_ref,
+    x_ref, new_ref, factor_ref, scale_ref, turn_ref, out_ref, load_sem, x_sem, sem,
+):
+    loads = [
+        pltpu.make_async_copy(source, target, load_sem.at[i])
+        for i, (source, target) in enumerate(
+            (
+                (turn_hbm, turn_ref),
+                (factor_hbm, factor_ref),
+                (scale_hbm, scale_ref),
+                (new_hbm, new_ref),
+            )
         )
-
-    kept_ref[...] = new_ref[...]
-    factor = factor_ref[...]
-    for lane in range(0, WIDTH, HEAD):
-        at = pl.ds(lane, HEAD)
-        out_ref[:, at] = (x_ref[:, at].astype(jnp.float32) * factor).astype(jnp.bfloat16)
-
-
-def finalize(positions, x, new, factor, scale):
-    def turned(i, pos):
-        return jnp.where(pos[0] > pos[RUN], 1 - i, i)
-
+    ]
+    strips = []
+    for i, start in enumerate(range(0, RUN, STRIP)):
+        for j in range(2):
+            at = pl.ds(j * RUN + start, STRIP)
+            strips.append(
+                pltpu.make_async_copy(x_hbm.at[at], x_ref.at[at], x_sem.at[2 * i + j])
+            )
+    for load in loads[:2] + strips + loads[2:]:
+        load.start()
+    for load in loads[:2]:
+        load.wait()
+    turned = jnp.broadcast_to(turn_ref[...], (STRIP, HEAD)) > 0.5
+    copies = []
+    for start in range(0, RUN, STRIP):
+        one, two = pl.ds(start, STRIP), pl.ds(RUN + start, STRIP)
+        low, high = factor_ref[one, :], factor_ref[two, :]
+        strips[len(copies)].wait()
+        strips[len(copies) + 1].wait()
+
+        def lanes(at, low, high, source, target, one=one, two=two):
+            a = source[one, at].astype(jnp.float32) * low
+            b = source[two, at].astype(jnp.float32) * high
+            target[one, at] = jnp.where(turned, b, a).astype(jnp.bfloat16)
+            target[two, at] = jnp.where(turned, a, b).astype(jnp.bfloat16)
+
+        for lane in range(0, D, HEAD):
+            lanes(pl.ds(lane, HEAD), low, high, x_ref, out_ref)
+        for at in (one, two):
+            copy = pltpu.make_async_copy(out_ref.at[at], out_hbm.at[at], sem.at[len(copies)])
+            copy.start()
+            copies.append(copy)
+        if start == 0:
+            for load in loads[2:]:
+                load.wait()
+        for lane in range(0, COLS, HEAD):
+            lanes(pl.ds(lane, HEAD), 1.0, 1.0, new_ref, kept_ref)
+    low = jnp.concatenate([scale_ref[i][:, :PART] for i in range(PER_HALF)], axis=1)
+    high = jnp.concatenate([scale_ref[i][:, :PART] for i in range(PER_HALF, PARTS)], axis=1)
+    flip = turn_ref[:, :RUN] > 0.5
+    row_ref[...] = jnp.concatenate(
+        [jnp.where(flip, high, low), jnp.where(flip, low, high)], axis=1
+    )
+    for copy in copies:
+        copy.wait()
+
+
+def finalize(*operands):
+    vmem = pl.BlockSpec(memory_space=pltpu.VMEM)
+    hbm = pl.BlockSpec(memory_space=pltpu.HBM)
     return pl.pallas_call(
         final_kernel,
         out_shape=(
@@ -687,31 +769,29 @@
             jax.ShapeDtypeStruct((1, TOK), jnp.float32),
             jax.ShapeDtypeStruct((TOK, COLS), jnp.bfloat16),
         ),
-        grid_spec=pltpu.PrefetchScalarGridSpec(
-            num_scalar_prefetch=1,
-            grid=(2, D // WIDTH),
-            in_specs=[
-                pl.BlockSpec((RUN, WIDTH), lambda i, j, pos: (turned(i, pos), j)),
-                pl.BlockSpec((RUN, COLS), lambda i, j, pos: (turned(i, pos), 0)),
-                pl.BlockSpec((RUN, HEAD), lambda i, j, pos: (turned(i, pos), 0)),
-                pl.BlockSpec((PARTS, 1, HEAD), lambda i, j, pos: (0, 0, 0)),
-            ],
-            out_specs=[
-                pl.BlockSpec((RUN, WIDTH), lambda i, j, pos: (i, j)),
-                pl.BlockSpec((1, TOK), lambda i, j, pos: (0, 0)),
-                pl.BlockSpec((RUN, COLS), lambda i, j, pos: (i, 0)),
-            ],
-        ),
-        compiler_params=pltpu.CompilerParams(vmem_limit_bytes=16 * 2**20),
+        in_specs=[hbm] * 5,
+        out_specs=[hbm, vmem, vmem],
+        scratch_shapes=[
+            pltpu.VMEM((TOK, D), jnp.bfloat16),
+            pltpu.VMEM((TOK, COLS), jnp.bfloat16),
+            pltpu.VMEM((TOK, HEAD), jnp.float32),
+            pltpu.VMEM((PARTS, 1, HEAD), jnp.float32),
+            pltpu.VMEM((1, HEAD), jnp.float32),
+            pltpu.VMEM((TOK, D), jnp.bfloat16),
+            pltpu.SemaphoreType.DMA((4,)),
+            pltpu.SemaphoreType.DMA((2 * RUN // STRIP,)),
+            pltpu.SemaphoreType.DMA((2 * RUN // STRIP,)),
+        ],
+        compiler_params=pltpu.CompilerParams(vmem_limit_bytes=VMEM_LIMIT),
         name="final",
-    )(positions, x, new, factor, scale)
+    )(*operands)
 
 
 def on_device(queries, key_vectors, value_vectors, positions, residual, norm_gain, out_weight):
-    shared, new, factor, scale = fused(
+    results = fused(
         positions, queries, key_vectors, value_vectors, out_weight, residual, norm_gain
     )
-    quantized, row, new_residual = finalize(positions, shared, new, factor, scale)
+    quantized, row, new_residual = finalize(*results)
     return (quantized, row.reshape(TOK), new_residual)
 
 

time: 87 us -> 72.4 us (0.83)
  local copies, waits for them, and re-layouts: 8.55 us -> 0 us
  Pallas kernels: 77.4 us -> 71.5 us
    unnamed x14 -> x0, local copies, waits for them, and re-layouts: 8.55 us -> none
    pallas_call x1, Pallas kernels: 73.3 us -> 67.5 us  [fused(): pl.pallas_call(fused_kernel, out_shape=(jax.ShapeDtypeStruct((TOK, D), bf...]
where the time goes in v4:
time: 72.4 us; the launch traced here: 72.3 us
  Pallas kernels  71.5 us (99%)
  between operations  0.8 us (1%)
    pallas_call x1, Pallas kernels, fused(): pl.pallas_call(fused_kernel, out_shape=(jax.ShapeDtypeStruct((TOK, D), bf...  67.5 us
    pallas_call x1, Pallas kernels, finalize(): pl.pallas_call(final_kernel, out_shape=(jax.ShapeDtypeStruct((TOK, D), jn...  3.97 us

profile of v4, /device:TPU:1, one launch (start us, length us, event | category | flops | bytes accessed | tf_op | source)
XLA Modules:
  0.0 72.3 jit_solution(18131274152102776260)
XLA Ops:
  0.6 67.5 %fused.1 = (bf16[192,6144]{1,0:T(8,128)(2,1)}, bf16[192,768]{1,0:T(8,128)(2,1)}, f32[192,128]{1,0:T(8,128)}, f32[4,1,128]{2,1,0:T(1,128)}, f32[1,128]{1,0:T(1,128)}) custom-call(s32[192]{0:T(256)} %pos_hbm.1, bf16[192,768]{1,0:T(8,128)(2,1)} %q_hbm.1, bf16[192,128]{1,0:T(8,128)(2,1)} %k_hbm.1, bf16[192,128]{1,0:T(8,128)(2,1)} %v_hbm.1, ...), custom_call_target="tpu_custom_call" | custom-call | tf_op jit(solution)/shard_map/fused/pallas_call | solution.py:642
  68.2 4.0 %final.1 = (bf16[192,6144]{1,0:T(8,128)(2,1)}, f32[1,192]{1,0:T(1,128)}, bf16[192,768]{1,0:T(8,128)(2,1)}) custom-call(bf16[192,6144]{1,0:T(8,128)(2,1)} %get-tuple-element.11.x_hbm, bf16[192,768]{1,0:T(8,128)(2,1)} %get-tuple-element.12.new_hbm, f32[192,128]{1,0:T(8,128)} %get-tuple-element.13.factor_hbm, f32[4,1,128]{2,1,0:T(1,128)} %get-tuple-element.14.scale_hbm, ...), custom_call_target="tpu_custom_call" | custom-call | tf_op jit(solution)/shard_map/final/pallas_call | solution.py:765

commit v5 on v4

--- a/solution.py
+++ b/solution.py
@@ -27,6 +27,9 @@
 PARTS = 2 * PER_HALF
 PART = TOK // PARTS
 NEG = -1e30
+SUM_DIRECT = ()
+SHARE_DIRECT = ()
+BEFORE_LO = [("pass_up", PARTS - 1), ("pass_down", PARTS - 1)]
 EXP_SCALE = math.log2(math.e) / math.sqrt(HEAD)
 MESH = pl.DeviceIdType.MESH
 
@@ -45,7 +48,7 @@
 for _k in DIRECT:
     REACH[_k] = (2, 1) + REACH[_k][2:]
 FAR = (2, 1, -1, 0)
-X_PLUS, X_MINUS, Z_PLUS, Z_MINUS, Y_PLUS, Y_MINUS, PAIR, X_FAR = range(8)
+X_PLUS, X_MINUS, Z_PLUS, Z_MINUS, Y_PLUS, Y_MINUS, PAIR, X_FAR, Y_FAR = range(9)
 (
     UP_RELAY, UP_DIRECT, UP_LAST, DOWN_RELAY, DOWN_DIRECT, DOWN_LAST,
     X_UP, X_DOWN, X_UP_FAR, X_DOWN_FAR,
@@ -129,7 +132,15 @@
         for slot, step in enumerate(FAR):
             sends = []
             for part in parts:
-                if step == 2:
+                if part in SUM_DIRECT:
+                    pairs, link = {
+                        2: ((UP_RELAY, DOWN_RELAY), Y_FAR),
+                        1: ((UP_LAST, UP_DIRECT), Y_PLUS),
+                        -1: ((DOWN_DIRECT, DOWN_LAST), Y_MINUS),
+                        0: ((), Y_PLUS),
+                    }[step]
+                    sends += [((part, event), link, PART_US) for event in pairs]
+                elif step == 2:
                     sends += [((part, UP_RELAY), Y_PLUS, PART_US), ((part, DOWN_RELAY), Y_MINUS, PART_US)]
                 elif step == 1:
                     sends += [((part, UP_DIRECT), Y_PLUS, PART_US)]
@@ -138,33 +149,52 @@
             needs = [("attended", half)] if slot == 0 else [("project", half, slot - 1)]
             tasks[("project", half, slot)] = (9 + late, [("att", half)], needs, PROJECT_US, sends)
         for part in parts:
-            tasks[("pass_up", part)] = (
-                4 + late, [(part, UP_RELAY)], [("project", half, 1)], 0.1,
-                [((part, UP_LAST), Y_PLUS, PART_US)],
-            )
-            tasks[("pass_down", part)] = (
-                4 + late, [(part, DOWN_RELAY)], [("project", half, 2)], 0.1,
-                [((part, DOWN_LAST), Y_MINUS, PART_US)],
-            )
+            direct = part in SUM_DIRECT
+            if not direct:
+                tasks[("pass_up", part)] = (
+                    4 + late, [(part, UP_RELAY)], [("project", half, 1)], 0.1,
+                    [((part, UP_LAST), Y_PLUS, PART_US)],
+                )
+                tasks[("pass_down", part)] = (
+                    4 + late, [(part, DOWN_RELAY)], [("project", half, 2)], 0.1,
+                    [((part, DOWN_LAST), Y_MINUS, PART_US)],
+                )
             tasks[("finish", part)] = (
                 6 + late,
-                [(part, e) for e in (UP_DIRECT, DOWN_DIRECT, UP_LAST, DOWN_LAST)],
+                [
+                    (part, e)
+                    for e in (UP_DIRECT, DOWN_DIRECT, UP_LAST, DOWN_LAST)
+                    + ((UP_RELAY, DOWN_RELAY) if direct else ())
+                ],
                 [("project", half, 3)],
                 0.4,
+                [((part, "stats"), PAIR, 0.1)],
+            )
+            tasks[("publish", part)] = (
+                6.1 + late,
+                [],
+                [("finish", part)] + (BEFORE_LO if half == LO else []),
+                0.02,
                 [
                     ((part, X_UP), Y_PLUS, 2 * PART_US),
                     ((part, X_DOWN), Y_MINUS, 2 * PART_US),
                     ((part, X_PAIR), PAIR, 0.15),
-                    ((part, "stats"), PAIR, 0.1),
-                ],
+                ]
+                + (
+                    [((part, X_UP_FAR), Y_FAR, PART_US), ((part, X_DOWN_FAR), Y_FAR, PART_US)]
+                    if part in SHARE_DIRECT
+                    else []
+                ),
             )
             tasks[("share_up", part)] = (
                 5 + late, [(part, X_UP)], [], 0.03,
-                [((part, X_UP_FAR), Y_PLUS, PART_US), ((part, X_PAIR_UP), PAIR, 0.15)],
+                [((part, X_PAIR_UP), PAIR, 0.15)]
+                + ([] if part in SHARE_DIRECT else [((part, X_UP_FAR), Y_PLUS, PART_US)]),
             )
             tasks[("share_down", part)] = (
                 5 + late, [(part, X_DOWN)], [], 0.03,
-                [((part, X_DOWN_FAR), Y_MINUS, PART_US), ((part, X_PAIR_DOWN), PAIR, 0.15)],
+                [((part, X_PAIR_DOWN), PAIR, 0.15)]
+                + ([] if part in SHARE_DIRECT else [((part, X_DOWN_FAR), Y_MINUS, PART_US)]),
             )
             tasks[("far_up", part)] = (
                 5 + late, [(part, X_UP_FAR)], [], 0.03, [((part, X_PAIR_UP_FAR), PAIR, 0.1)]
@@ -175,14 +205,14 @@
             tasks[("scales", part)] = (
                 50,
                 [(part, "stats")],
-                [(far, every) for far in ("far_up", "far_down") for every in range(PARTS)],
+                [("publish", part)],
                 0.3,
                 [],
             )
             pairs = (X_PAIR, X_PAIR_UP, X_PAIR_DOWN, X_PAIR_UP_FAR, X_PAIR_DOWN_FAR)
             tasks[("collect", part)] = (60, [(part, e) for e in pairs], [], 0.02, [])
 
-    free = [0.0] * 8
+    free = [0.0] * 9
     when = {}
     order, done = [], set()
     left = dict(tasks)
@@ -208,13 +238,14 @@
         done.add(task)
         order.append((task, now))
         for arrival, link, took in sends:
-            if link == X_FAR:
-                free[X_PLUS] = max(free[X_PLUS], now) + took
-                free[X_MINUS] = max(free[X_MINUS], now) + took
-                when[arrival] = max(free[X_PLUS], free[X_MINUS]) + HOP_US + 0.7
+            if link in (X_FAR, Y_FAR):
+                ways = (X_PLUS, X_MINUS) if link == X_FAR else (Y_PLUS, Y_MINUS)
+                for way in ways:
+                    free[way] = max(free[way], now) + took
+                when[arrival] = max(free[way] for way in ways) + HOP_US + 0.7
                 continue
             free[link] = max(free[link], now) + took
-            hop = 3.0 if arrival[-1] == "stats" else PAIR_US if link == PAIR else HOP_US
+            hop = 7.0 if arrival[-1] == "stats" else PAIR_US if link == PAIR else HOP_US
             when[arrival] = free[link] + hop
     return order, now
 
@@ -288,10 +319,10 @@
 
 def fused_kernel(
     pos_hbm, q_hbm, k_hbm, v_hbm, w_ref, residual_hbm, gain_hbm,
-    x_hbm, new_ref, factor_ref, scale_ref, turn_ref,
-    x_ref, pos_ref, q_ref, k_ref, v_ref, residual_ref, gain_ref, own, own_id, kv, ids, queries, m_ref, l_ref, acc_ref,
+    x_hbm, new_hbm, factor_hbm, scale_hbm, turn_hbm,
+    x_ref, new_ref, factor_ref, scale_ref, turn_ref, pos_ref, q_ref, k_ref, v_ref, residual_ref, gain_ref, own, own_id, kv, ids, queries, m_ref, l_ref, acc_ref,
     weights, attended, mine, outgoing, relayed, got, stats,
-    store_sem, early_sem, load_sem, send, recv, w_send, w_recv, att_send, att_recv,
+    store_sem, small_sem, early_sem, load_sem, send, recv, w_send, w_recv, att_send, att_recv,
     part_send, part_recv, stat_send, stat_recv,
 ):
     seq = lax.axis_index("seq")
@@ -309,6 +340,7 @@
         (seq, lax.rem(tp + 6, N_TP)),
         (seq, y * 2 + 1 - core),
         (z * NX + lax.rem(x + 2, NX), tp),
+        (seq, lax.rem(tp + 4, N_TP)),
     )
 
     def columns(step, parity, first=0, width=COLS):
@@ -317,6 +349,11 @@
 
     sent = []
     stores = []
+
+    def keep(source, target, sem):
+        store = pltpu.make_async_copy(source, target, sem)
+        store.start()
+        stores.append(store)
 
     def remote(source, target, send_sem, recv_sem, peer):
         return pltpu.make_async_remote_copy(
@@ -484,7 +521,15 @@
         outgoing[slot, pl.ds(half * RUN, RUN), :] = product.astype(jnp.bfloat16)
         for part in range(half * PER_HALF, (half + 1) * PER_HALF):
             here = outgoing.at[slot, rows(part)]
-            if step == 2:
+            if part in SUM_DIRECT:
+                (first, second), peer = {
+                    2: ((UP_RELAY, DOWN_RELAY), Y_FAR),
+                    1: ((UP_LAST, UP_DIRECT), Y_PLUS),
+                    -1: ((DOWN_DIRECT, DOWN_LAST), Y_MINUS),
+                }[step]
+                send_part(part, first, here.at[:, left], slab(first, part), peer)
+                send_part(part, second, here.at[:, right], slab(second, part), peer)
+            elif step == 2:
                 send_part(part, UP_RELAY, here.at[:, left], slab(UP_RELAY, part), Y_PLUS)
                 send_part(part, DOWN_RELAY, here.at[:, right], slab(DOWN_RELAY, part), Y_MINUS)
             elif step == 1:
@@ -515,27 +560,27 @@
         inside = (part % PER_HALF) * PART
         one, two = pl.ds(inside, PART), pl.ds(RUN + inside, PART)
         turned = swapped[0:PART]
-        for first, direct, last in ((0, DOWN_DIRECT, UP_LAST), (HALF, UP_DIRECT, DOWN_LAST)):
-            await_part(part, direct, slab(direct, part))
-            await_part(part, last, slab(last, part))
+        for first, *events in (
+            (0, DOWN_DIRECT, UP_LAST, UP_RELAY),
+            (HALF, UP_DIRECT, DOWN_LAST, DOWN_RELAY),
+        ):
+            events = events if part in SUM_DIRECT else events[:2]
+            for event in events:
+                await_part(part, event, slab(event, part))
             for lane in range(0, HALF, HEAD):
                 here = pl.ds(first + lane, HEAD)
                 there = pl.ds(lane, HEAD)
                 low = residual_ref[one, here].astype(jnp.float32)
                 high = residual_ref[two, here].astype(jnp.float32)
                 old = jnp.where(turned, high, low) if half_of == LO else jnp.where(turned, low, high)
-                summed = (
-                    mine[at, here]
-                    + slab(direct, part)[:, there].astype(jnp.float32)
-                    + slab(last, part)[:, there].astype(jnp.float32)
-                    + old
-                )
+                summed = mine[at, here] + old
+                for event in events:
+                    summed = summed + slab(event, part)[:, there].astype(jnp.float32)
                 new_ref[at, here] = summed.astype(jnp.bfloat16)
                 gained = summed * gain_ref[:, here]
                 x_ref[at, columns(0, core, first + lane, HEAD)] = gained.astype(jnp.bfloat16)
                 squares = squares + summed * summed
                 peak = jnp.maximum(peak, jnp.abs(gained))
-        block = x_ref.at[at, columns(0, core)]
         lane = lax.broadcasted_iota(jnp.int32, (PART, HEAD), 1)
         both = jnp.where(
             lane == 0,
@@ -545,9 +590,6 @@
         if PART < HEAD:
             both = jnp.concatenate([both, jnp.zeros((HEAD - PART, HEAD), jnp.float32)], axis=0)
         stats[part, tp] = jnp.transpose(both)[0:8, :]
-        send_part(part, X_UP, block, block, Y_PLUS)
-        send_part(part, X_DOWN, block, block, Y_MINUS)
-        send_part(part, X_PAIR, block, block, PAIR)
         for step in range(1, N_TP):
             ship(
                 stats.at[part, tp],
@@ -556,6 +598,20 @@
                 stat_recv.at[part, step],
                 (seq, lax.rem(tp + step, N_TP)),
             )
+
+    def publish(part):
+        at = rows(part)
+        keep(new_ref.at[at], new_hbm.at[at], small_sem.at[2, part])
+        if part == 0:
+            keep(turn_ref, turn_hbm, early_sem.at[4])
+        block = x_ref.at[at, columns(0, core)]
+        send_part(part, X_UP, block, block, Y_PLUS)
+        send_part(part, X_DOWN, block, block, Y_MINUS)
+        if part in SHARE_DIRECT:
+            for event, first in ((X_UP_FAR, 0), (X_DOWN_FAR, HALF)):
+                half = x_ref.at[at, columns(0, core, first, HALF)]
+                send_part(part, event, half, half, Y_FAR)
+        send_part(part, X_PAIR, block, block, PAIR)
 
     def share(part, way):
         arrival, far, pair, step, first, peer = (
@@ -565,8 +621,9 @@
         at = rows(part)
         block = x_ref.at[at, columns(step, core)]
         await_part(part, arrival, block)
-        half = x_ref.at[at, columns(step, core, first, HALF)]
-        send_part(part, far, half, half, peer)
+        if part not in SHARE_DIRECT:
+            half = x_ref.at[at, columns(step, core, first, HALF)]
+            send_part(part, far, half, half, peer)
         send_part(part, pair, block, block, PAIR)
 
     def share_far(part, way):
@@ -592,6 +649,8 @@
         scale_ref[part] = scale
         factor = jnp.transpose(jnp.broadcast_to(root / scale, (HEAD, HEAD)))
         factor_ref[rows(part), :] = factor[0:PART, :]
+        keep(scale_ref.at[part], scale_hbm.at[part], small_sem.at[0, part])
+        keep(factor_ref.at[rows(part)], factor_hbm.at[rows(part)], small_sem.at[1, part])
 
     def collect(part):
         at = rows(part)
@@ -604,9 +663,7 @@
             (X_PAIR_DOWN_FAR, 2, HALF, HALF),
         ):
             await_part(part, event, x_ref.at[at, columns(step, other, first, width)])
-        store = pltpu.make_async_copy(x_ref.at[at], x_hbm.at[at], store_sem.at[part])
-        store.start()
-        stores.append(store)
+        keep(x_ref.at[at], x_hbm.at[at], store_sem.at[part])
 
     emit = {
         "relay": relay,
@@ -619,6 +676,7 @@
         "pass_up": lambda part: pass_on(part, 0),
         "pass_down": lambda part: pass_on(part, 1),
         "finish": finish,
+        "publish": publish,
         "share_up": lambda part: share(part, 0),
         "share_down": lambda part: share(part, 1),
         "far_up": lambda part: share_far(part, 0),
@@ -635,7 +693,6 @@
 
 
 def fused(positions, queries, keys, values, out_weight, residual, gain):
-    vmem = pl.BlockSpec(memory_space=pltpu.VMEM)
     hbm = pl.BlockSpec(memory_space=pltpu.HBM)
     bf16, f32 = jnp.bfloat16, jnp.float32
     dma = pltpu.SemaphoreType.DMA
@@ -649,9 +706,13 @@
             jax.ShapeDtypeStruct((1, HEAD), f32),
         ),
         in_specs=[hbm] * 7,
-        out_specs=[hbm] + [vmem] * 4,
+        out_specs=[hbm] * 5,
         scratch_shapes=[
             pltpu.VMEM((TOK, D), bf16),
+            pltpu.VMEM((TOK, COLS), bf16),
+            pltpu.VMEM((TOK, HEAD), f32),
+            pltpu.VMEM((PARTS, 1, HEAD), f32),
+            pltpu.VMEM((1, HEAD), f32),
             pltpu.SMEM((TOK,), jnp.int32),
             pltpu.VMEM((TOK, COLS), bf16),
             pltpu.VMEM((TOK, HEAD), bf16),
@@ -674,7 +735,8 @@
             pltpu.VMEM((6, TOK, HALF), bf16),
             pltpu.VMEM((PARTS, N_TP, 8, HEAD), f32),
             dma((PARTS,)),
-            dma((4,)),
+            dma((3, PARTS)),
+            dma((5,)),
             dma((6,)),
             dma((N_EVENTS,)),
             dma((N_EVENTS,)),

time: 72.4 us -> 71.6 us (0.989)
  Pallas kernels: 71.5 us -> 70.7 us
    pallas_call x1, Pallas kernels: 67.5 us -> 66.7 us  [fused(): pl.pallas_call(fused_kernel, out_shape=(jax.ShapeDtypeStruct((TOK, D), bf...]
where the time goes in v5:
time: 71.6 us; the launch traced here: 71.5 us
  Pallas kernels  70.7 us (99%)
  between operations  0.8 us (1%)
    pallas_call x1, Pallas kernels, fused(): pl.pallas_call(fused_kernel, out_shape=(jax.ShapeDtypeStruct((TOK, D), bf...  66.7 us
    pallas_call x1, Pallas kernels, finalize(): pl.pallas_call(final_kernel, out_shape=(jax.ShapeDtypeStruct((TOK, D), jn...  3.97 us

profile of v5, /device:TPU:1, one launch (start us, length us, event | category | flops | bytes accessed | tf_op | source)
XLA Modules:
  0.0 71.5 jit_solution(4804479622643833816)
XLA Ops:
  0.6 66.7 %fused.1 = (bf16[192,6144]{1,0:T(8,128)(2,1)}, bf16[192,768]{1,0:T(8,128)(2,1)}, f32[192,128]{1,0:T(8,128)}, f32[4,1,128]{2,1,0:T(1,128)}, f32[1,128]{1,0:T(1,128)}) custom-call(s32[192]{0:T(256)} %pos_hbm.1, bf16[192,768]{1,0:T(8,128)(2,1)} %q_hbm.1, bf16[192,128]{1,0:T(8,128)(2,1)} %k_hbm.1, bf16[192,128]{1,0:T(8,128)(2,1)} %v_hbm.1, ...), custom_call_target="tpu_custom_call" | custom-call | tf_op jit(solution)/shard_map/fused/pallas_call | solution.py:699
  67.3 4.0 %final.1 = (bf16[192,6144]{1,0:T(8,128)(2,1)}, f32[1,192]{1,0:T(1,128)}, bf16[192,768]{1,0:T(8,128)(2,1)}) custom-call(bf16[192,6144]{1,0:T(8,128)(2,1)} %get-tuple-element.11.x_hbm, bf16[192,768]{1,0:T(8,128)(2,1)} %get-tuple-element.12.new_hbm, f32[192,128]{1,0:T(8,128)} %get-tuple-element.13.factor_hbm, f32[4,1,128]{2,1,0:T(1,128)} %get-tuple-element.14.scale_hbm, ...), custom_call_target="tpu_custom_call" | custom-call | tf_op jit(solution)/shard_map/final/pallas_call | solution.py:827

commit v6 on v5

--- a/solution.py
+++ b/solution.py
@@ -23,7 +23,7 @@
 CHUNK = 2 * RUN
 COLS = HEADS * HEAD
 HALF = COLS // 2
-PER_HALF = 2
+PER_HALF = 1
 PARTS = 2 * PER_HALF
 PART = TOK // PARTS
 NEG = -1e30
@@ -47,6 +47,7 @@
 DIRECT = (K_LO, K_HI, RUN_ID, V_LO, V_HI)
 for _k in DIRECT:
     REACH[_k] = (2, 1) + REACH[_k][2:]
+REACH[RUN_ID] = (2, 1, 0, 0)
 FAR = (2, 1, -1, 0)
 X_PLUS, X_MINUS, Z_PLUS, Z_MINUS, Y_PLUS, Y_MINUS, PAIR, X_FAR, Y_FAR = range(9)
 (
@@ -87,12 +88,27 @@
     ]
 
 
-EVENT_ID = {key: i for i, key in enumerate(key for kind in KINDS for key in moves(kind))}
+def onward(mz):
+    steps = []
+    if 0 <= mz < 4:
+        steps.append((mz + 1, Z_PLUS))
+    if -3 < mz <= 0:
+        steps.append((mz - 1, Z_MINUS))
+    return steps
+
+
+EVENT_ID = {
+    key: i
+    for i, key in enumerate(
+        [key for kind in KINDS for key in moves(kind)]
+        + [("ids", mz) for mz in range(-3, 5) if mz]
+    )
+}
 N_EVENTS = len(EVENT_ID)
 UNIT_US = 0.6
 PROJECT_US = 0.5
-HOP_US = 2.3
-PAIR_US = 1.1
+HOP_US = 2.9
+PAIR_US = 1.5
 PIECE_US = 0.55
 PART_US = 1.6 * PART / RUN
 
@@ -109,10 +125,17 @@
     start = [("relay", kind, 0, 0) for kind in KINDS]
     tasks[("diagonal",)] = (2, [], start, 0.8, [])
 
+    for mz in range(-3, 5):
+        needs = [("relay",) + key for key in moves(RUN_ID)] if mz == 0 else []
+        tasks[("ids", mz)] = (
+            0, [("ids", mz)] if mz else [], needs, 0.03,
+            [(("ids", step), link, 0.05) for step, link in onward(mz)],
+        )
+
     def group_keys(kinds, dz):
         return [k for kind in kinds for k in moves(kind) if (k[2] - dz) % NZ == 0]
 
-    lo_kinds, hi_kinds = (K_LO, V_LO, RUN_ID), (K_HI, V_HI)
+    lo_kinds, hi_kinds = (K_LO, V_LO), (K_HI, V_HI)
     fins = {LO: [("diagonal",)], HI: [("diagonal",)]}
     for i, dz in enumerate((0, 1, -1, 2, -2, 3, -3, 4)):
         for name, kinds, half, base in (
@@ -120,9 +143,9 @@
             ("hi_lo", lo_kinds, HI, 40),
             ("hi_hi", hi_kinds, HI, 41),
         ):
-            keys = group_keys(kinds, dz) + (group_keys((RUN_ID,), dz) if name == "hi_hi" else [])
+            keys = group_keys(kinds, dz)
             task = (name, dz)
-            relays = [("relay",) + k for k in keys]
+            relays = [("relay",) + k for k in keys] + [("ids", dz)]
             tasks[task] = (base + 0.1 * i, [], relays + [("diagonal",)], UNIT_US, [])
             fins[half].append(task)
     for half in (LO, HI):
@@ -440,6 +463,15 @@
         for child in children(kind, mx, mz):
             event = EVENT_ID[child[:3]]
             ship(source, here, send.at[event], recv.at[event], peers[child[3]])
+
+    def pass_ids(mz):
+        here = ids.at[pl.ds(lax.rem(z + 2 * NZ - mz, NZ) * NX, NX)]
+        if mz:
+            event = EVENT_ID[("ids", mz)]
+            arrive(here, send.at[event], recv.at[event])
+        for step, link in onward(mz):
+            event = EVENT_ID[("ids", step)]
+            ship(here, here, send.at[event], recv.at[event], peers[link])
 
     def diagonal():
         for slot in range(4):
@@ -667,6 +699,7 @@
 
     emit = {
         "relay": relay,
+        "ids": pass_ids,
         "diagonal": diagonal,
         "lo_lo": lambda dz: unit(dz, LO, True),
         "hi_lo": lambda dz: unit(dz, HI, True),

time: 71.6 us -> 70.4 us (0.983)
  Pallas kernels: 70.7 us -> 69.4 us
    pallas_call x1, Pallas kernels: 66.7 us -> 65.5 us  [fused(): pl.pallas_call(fused_kernel, out_shape=(jax.ShapeDtypeStruct((TOK, D), bf...]
where the time goes in v6:
time: 70.4 us; the launch traced here: 70.2 us
  Pallas kernels  69.4 us (99%)
  between operations  0.8 us (1%)
    pallas_call x1, Pallas kernels, fused(): pl.pallas_call(fused_kernel, out_shape=(jax.ShapeDtypeStruct((TOK, D), bf...  65.5 us
    pallas_call x1, Pallas kernels, finalize(): pl.pallas_call(final_kernel, out_shape=(jax.ShapeDtypeStruct((TOK, D), jn...  3.94 us

profile of v6, /device:TPU:1, one launch (start us, length us, event | category | flops | bytes accessed | tf_op | source)
XLA Modules:
  0.0 70.2 jit_solution(14129915133356755648)
XLA Ops:
  0.6 65.5 %fused.1 = (bf16[192,6144]{1,0:T(8,128)(2,1)}, bf16[192,768]{1,0:T(8,128)(2,1)}, f32[192,128]{1,0:T(8,128)}, f32[2,1,128]{2,1,0:T(1,128)}, f32[1,128]{1,0:T(1,128)}) custom-call(s32[192]{0:T(256)} %pos_hbm.1, bf16[192,768]{1,0:T(8,128)(2,1)} %q_hbm.1, bf16[192,128]{1,0:T(8,128)(2,1)} %k_hbm.1, bf16[192,128]{1,0:T(8,128)(2,1)} %v_hbm.1, ...), custom_call_target="tpu_custom_call" | custom-call | tf_op jit(solution)/shard_map/fused/pallas_call | solution.py:732
  66.1 3.9 %final.1 = (bf16[192,6144]{1,0:T(8,128)(2,1)}, f32[1,192]{1,0:T(1,128)}, bf16[192,768]{1,0:T(8,128)(2,1)}) custom-call(bf16[192,6144]{1,0:T(8,128)(2,1)} %get-tuple-element.11.x_hbm, bf16[192,768]{1,0:T(8,128)(2,1)} %get-tuple-element.12.new_hbm, f32[192,128]{1,0:T(8,128)} %get-tuple-element.13.factor_hbm, f32[2,1,128]{2,1,0:T(1,128)} %get-tuple-element.14.scale_hbm, ...), custom_call_target="tpu_custom_call" | custom-call | tf_op jit(solution)/shard_map/final/pallas_call | solution.py:860

commit v7 on v6

--- a/solution.py
+++ b/solution.py
@@ -120,9 +120,9 @@
         for key in [(kind, 0, 0)] + moves(kind):
             sends = [(child[:3], child[3], took) for child in children(*key)]
             own = key[1:] == (0, 0)
-            rank = (0 if kind in (K_LO, V_LO, RUN_ID) else 1) + (-2 if own else 0)
-            tasks[("relay",) + key] = (rank, [] if own else [key], [], 0.03, sends)
-    start = [("relay", kind, 0, 0) for kind in KINDS]
+            rank = (0 if kind in (K_LO, V_LO, RUN_ID) else 1) + (-2 if own and kind not in (K_HI, V_HI) else 0)
+            tasks[("relay",) + key] = (rank, [] if own else [key], ([("relay", K_LO, 0, 2)]) if own and kind in (K_HI, V_HI) else [], 0.03, sends)
+    start = [("relay", kind, 0, 0) for kind in KINDS[:3]]
     tasks[("diagonal",)] = (2, [], start, 0.8, [])
 
     for mz in range(-3, 5):

time: 70.4 us -> 68.9 us (0.979)
  Pallas kernels: 69.4 us -> 68 us
    pallas_call x1, Pallas kernels: 65.5 us -> 64.1 us  [fused(): pl.pallas_call(fused_kernel, out_shape=(jax.ShapeDtypeStruct((TOK, D), bf...]
where the time goes in v7:
time: 68.9 us; the launch traced here: 68.8 us
  Pallas kernels  68 us (99%)
  between operations  0.8 us (1%)
    pallas_call x1, Pallas kernels, fused(): pl.pallas_call(fused_kernel, out_shape=(jax.ShapeDtypeStruct((TOK, D), bf...  64.1 us
    pallas_call x1, Pallas kernels, finalize(): pl.pallas_call(final_kernel, out_shape=(jax.ShapeDtypeStruct((TOK, D), jn...  3.94 us

profile of v7, /device:TPU:1, one launch (start us, length us, event | category | flops | bytes accessed | tf_op | source)
XLA Modules:
  0.0 68.8 jit_solution(18444783063065199478)
XLA Ops:
  0.6 64.1 %fused.1 = (bf16[192,6144]{1,0:T(8,128)(2,1)}, bf16[192,768]{1,0:T(8,128)(2,1)}, f32[192,128]{1,0:T(8,128)}, f32[2,1,128]{2,1,0:T(1,128)}, f32[1,128]{1,0:T(1,128)}) custom-call(s32[192]{0:T(256)} %pos_hbm.1, bf16[192,768]{1,0:T(8,128)(2,1)} %q_hbm.1, bf16[192,128]{1,0:T(8,128)(2,1)} %k_hbm.1, bf16[192,128]{1,0:T(8,128)(2,1)} %v_hbm.1, ...), custom_call_target="tpu_custom_call" | custom-call | tf_op jit(solution)/shard_map/fused/pallas_call | solution.py:732
  64.7 3.9 %final.1 = (bf16[192,6144]{1,0:T(8,128)(2,1)}, f32[1,192]{1,0:T(1,128)}, bf16[192,768]{1,0:T(8,128)(2,1)}) custom-call(bf16[192,6144]{1,0:T(8,128)(2,1)} %get-tuple-element.11.x_hbm, bf16[192,768]{1,0:T(8,128)(2,1)} %get-tuple-element.12.new_hbm, f32[192,128]{1,0:T(8,128)} %get-tuple-element.13.factor_hbm, f32[2,1,128]{2,1,0:T(1,128)} %get-tuple-element.14.scale_hbm, ...), custom_call_target="tpu_custom_call" | custom-call | tf_op jit(solution)/shard_map/final/pallas_call | solution.py:860
